TPU v7x, 256 devices: a 8x8x2 block of a 8x8x16 slice. The times are simulated.
256 devices in a mesh: grp: 2 (over z), tp: 128 (over y, x, core).
Axes of the slice: x: 8, y: 8, z: 2, core: 2. Of those that a mesh axis runs over, the one named last changes fastest.
The devices are a block of a 8x8x16 slice.
Arguments:
- hidden: bfloat16 [1024, 16384], P('grp', 'tp'), parts along dimension 0, may hold values from -36 to 36
- norm_gain: float32 [16384], P('tp'), may hold values from 0.3 to 10, as said below
- prefix: int32 [2], P('grp'), parts along dimension 0, may hold values from 0 to 8192
- w_query: bfloat16 [16384, 16384], P(None, 'tp'), may hold values from -0.046875 to 0.046875
- w_kv: bfloat16 [2048, 16384], P('tp'), may hold values from -0.046875 to 0.046875
- w_scale: float32 [18432], P('tp'), may hold values from 0.25 to 4
Outputs:
- queries: bfloat16 [1024, 16384], P('grp', 'tp'), parts along dimension 0
- keys: bfloat16 [1024, 16384], P('grp', 'tp'), parts along dimension 0
- values: bfloat16 [1024, 16384], P('grp', 'tp'), parts along dimension 0
- payload: bfloat16 [1024, 16384], P('grp', 'tp'), parts along dimension 0
- row_scale: float32 [1024], P('grp'), parts along dimension 0
There are 2 independent parts, one for each index of `grp`. A program takes and returns all parts, laid end to end along the dimension named above; an argument that names none is the same for every part. Nothing has to cross between parts.
Inputs may be any that keep to these rules, and one draw needn't show every extreme that they name: `norm_gain`: positive.
All inputs are finite; a program needn't handle non-finite values. Where the computation divides by a largest or mean magnitude, that divisor is 1e-20 or more.
Results may differ from a plain program's by a relative error of at most 0.012.
Values may be sent and summed in bfloat16 or wider, within the bound.
No kernel may reach another device: no remote copies, remote signals or barrier semaphores. Data moves between devices by JAX's collectives and lax.ppermute only.
A program may use at most 64 MiB of HBM per device.

v0:
```python
import math

import jax
import jax.numpy as jnp
from jax import lax
from jax.experimental import pallas as pl
from jax.experimental.pallas import tpu as pltpu
from jax.sharding import PartitionSpec as P


HD = 128
KV_COLS_DEV = 8
norm_eps = 1e-05
tiny_eps = 1e-06
rope_base = 500000.0

VMEM = 24 * 2**20
RING_VMEM = 48 * 2**20

F32 = jnp.float32
BF16 = jnp.bfloat16
STAT = 16


def split2(v):
    hi = v.astype(BF16)
    return hi, (v - hi.astype(F32)).astype(BF16)


def prep_kernel(core, hidden, gain, keep, send):
    half = keep.shape[0] - STAT
    for out, which in ((keep, core[0]), (send, 1 - core[0])):
        h = hidden[pl.ds(pl.multiple_of(which * half, half), half), :].astype(F32)
        weighted = h * gain[...]
        out[:half, :] = weighted.astype(BF16)
        squares = jnp.sum(jnp.transpose(h * h), axis=0, keepdims=True)
        largest = jnp.max(jnp.transpose(jnp.abs(weighted)), axis=0, keepdims=True)
        rows = []
        for v in (squares, largest):
            for part in split2(v):
                part = part.astype(F32)
                rows += [part[:, :128], part[:, 128:]]
        rows.append(jnp.zeros((STAT - len(rows), 128), F32))
        out[half:, :] = jnp.concatenate(rows, axis=0).astype(BF16)


def combine_kernel(core, keep, recv, out):
    half = keep.shape[0] - STAT
    first = core[0] == 0
    mine, other = keep[:half, :], recv[:half, :]
    left = jnp.where(first, mine.astype(F32), other.astype(F32)).astype(BF16)
    right = jnp.where(first, other.astype(F32), mine.astype(F32)).astype(BF16)
    a, b = keep[half:, :].astype(F32), recv[half:, :].astype(F32)

    def wide(s, r):
        return jnp.concatenate([s[r : r + 1], s[r + 1 : r + 2]], axis=1)

    squares = (wide(a, 0) + wide(a, 2)) + (wide(b, 0) + wide(b, 2))
    largest = jnp.maximum(wide(a, 4) + wide(a, 6), wide(b, 4) + wide(b, 6))
    rows = [p.astype(F32) for v in (squares, largest) for p in split2(v)]
    rows.append(jnp.zeros((STAT - len(rows), rows[0].shape[1]), F32))
    stats = jnp.concatenate(rows, axis=0).astype(BF16)
    for s in range(out.shape[0]):
        out[s, :half, :128] = left
        out[s, :half, 128:] = right
        out[s, half:, :] = stats


def block_at(core, i, side):
    return jnp.where(core == 0, i, (i % side) * side + i // side)


def weights_kernel(info, wq, wo, w_all, w_buf, sems):
    n = w_buf.shape[0]
    hw = wq.shape[2]
    side = math.isqrt(n)

    def fetches(i):
        b = block_at(info[0], i, side)
        return (
            pltpu.make_async_copy(wq.at[b], w_buf.at[i, :, pl.ds(0, hw)], sems.at[0, i]),
            pltpu.make_async_copy(wo.at[b], w_buf.at[i, :, pl.ds(hw, hw)], sems.at[1, i]),
        )

    def store(i):
        return pltpu.make_async_copy(w_buf.at[i], w_all.at[i], sems.at[2, i])

    @pl.loop(0, n)
    def _(i):
        for c in fetches(i):
            c.start()

    @pl.loop(0, n)
    def _(i):
        for c in fetches(i):
            c.wait()
        store(i).start()

    @pl.loop(0, n)
    def _(i):
        store(i).wait()


def arrange_weights(info, wq, wo):
    n, kb, hw = wq.shape
    hbm = pl.BlockSpec(memory_space=pltpu.HBM)
    out = jax.ShapeDtypeStruct((n, kb, 2 * hw), BF16)
    return pl.pallas_call(
        weights_kernel,
        out_shape=out,
        in_specs=[pl.BlockSpec(memory_space=pltpu.SMEM), hbm, hbm],
        out_specs=hbm,
        scratch_shapes=[pltpu.VMEM(out.shape, out.dtype), pltpu.SemaphoreType.DMA((3, n))],
        compiler_params=pltpu.CompilerParams(vmem_limit_bytes=60 * 2**20),
        cost_estimate=pl.CostEstimate(flops=10**9, bytes_accessed=2 * 10**7, transcendentals=0),
    )(info, wq, wo)


def kv_weights_kernel(core, kv, ko, kv_all, kvscale):
    n, rows2, kb = kv_all.shape
    rows = rows2 // 2
    side = math.isqrt(n)
    for i in range(n):
        at = pl.ds(pl.multiple_of(block_at(core[0], i, side) * kb, kb), kb)
        kv_all[i, :rows, :] = kv[:, at]
        kv_all[i, rows:, :] = ko[:, at]
    width = kvscale.shape[1]

    def scales(ref):
        s = ref[:, n * kb : n * kb + 128].astype(F32)
        s = (s[:, 0:1] + s[:, 1:2]) + s[:, 2:3]
        return jnp.broadcast_to(s, (rows, width))

    m, o = scales(kv), scales(ko)
    first = core[0] == 0
    k = rows // 2
    for j, (lo, hi) in enumerate(((0, k), (k, 2 * k))):
        a, b = m[lo:hi], o[lo:hi]
        kvscale[2 * j * k : (2 * j + 1) * k, :] = jnp.where(first, a, b)
        kvscale[(2 * j + 1) * k : (2 * j + 2) * k, :] = jnp.where(first, b, a)


def high_kernel(gathered, high):
    n = gathered.shape[0] // 2
    half = gathered.shape[1] - STAT
    squares, largest = 0.0, 0.0
    for i in range(2 * n):
        s = gathered[i, half:, :].astype(F32)
        squares = squares + (s[0:1] + s[1:2])
        largest = jnp.maximum(largest, s[2:3] + s[3:4])
        if i >= n:
            high[(i - n) * half : (i - n + 1) * half, :] = gathered[i, :half, :]
    rows = [p.astype(F32) for v in (squares, largest) for p in split2(v)]
    rows.append(jnp.zeros((STAT - len(rows), rows[0].shape[1]), F32))
    high[n * half :, :] = jnp.concatenate(rows, axis=0).astype(BF16)


def kv_rows(xs, kvs, kv_in, st_in):
    half = kv_in.shape[1]
    total = kv_in[...]
    squares, largest = st_in[0:1, :], st_in[1:2, :]
    for x, w in zip(xs, kvs):
        n = len(w)
        for i in range(n):
            total = total + lax.dot_general(
                w[i],
                x[i * half : (i + 1) * half, :],
                (((1,), (1,)), ((), ())),
                preferred_element_type=F32,
            )
        if x.shape[0] > n * half:
            s = x[n * half :, :].astype(F32)
            squares = squares + (s[0:1] + s[1:2])
            largest = jnp.maximum(largest, s[2:3] + s[3:4])
    return total, squares, largest


def q_sum(xs, ws, q_in):
    half = q_in.shape[0]
    total = q_in[...]
    for x, w in zip(xs, ws):
        for i in range(len(w)):
            total = total + jnp.dot(
                x[i * half : (i + 1) * half, :],
                w[i],
                preferred_element_type=F32,
            )
    return total


def places_of(info, shifts, whole, n):
    side = math.isqrt(whole.shape[0])
    return [lax.rem(info[1] + (side - s % side), side) * side + k * n for s, k in shifts]


def blocks_from(info, shifts, whole, n):
    return [[whole[p + j] for j in range(n)] for p in places_of(info, shifts, whole, n)]


def fetch(info, shifts, w_all, w_buf, sems):
    n = w_buf.shape[1]
    copies = [
        pltpu.make_async_copy(w_all.at[pl.ds(p, n)], w_buf.at[i], sems.at[i])
        for i, p in enumerate(places_of(info, shifts, w_all, n))
    ]
    for c in copies:
        c.start()
    return copies


def ahead_kernel(shifts, info, w_all, w_next, sems):
    for c in fetch(info, shifts, w_all, w_next, sems):
        c.wait()


def first_weights(info, shifts, w_all, n):
    m = len(shifts)
    hbm = pl.BlockSpec(memory_space=pltpu.HBM)
    return pl.pallas_call(
        lambda *refs: ahead_kernel(shifts, *refs),
        out_shape=jax.ShapeDtypeStruct((m, n) + w_all.shape[1:], BF16),
        in_specs=[pl.BlockSpec(memory_space=pltpu.SMEM), hbm],
        out_specs=pl.BlockSpec(memory_space=pltpu.VMEM),
        scratch_shapes=[pltpu.SemaphoreType.DMA((m,))],
        compiler_params=pltpu.CompilerParams(vmem_limit_bytes=RING_VMEM),
        cost_estimate=pl.CostEstimate(flops=10**8, bytes_accessed=10**6, transcendentals=0),
    )(info, w_all)


def matmul_kernel(shifts, next_shifts, info, *refs):
    m = len(shifts)
    xs, w_now, w_all, kv_all = refs[:m], *refs[m : m + 3]
    q_out, kv_out, st_out, w_next, sems = refs[-5:]
    copies = fetch(info, next_shifts, w_all, w_next, sems)
    if len(refs) == m + 8:
        q_in, kv_in, st_in = q_out, kv_out, st_out
        for out in (q_out, kv_out, st_out):
            out[...] = jnp.zeros_like(out)
    else:
        q_in, kv_in, st_in = refs[m + 3 : m + 6]
    n = w_now.shape[1]
    kvs = blocks_from(info, shifts, kv_all, n)
    total, squares, largest = kv_rows(xs, kvs, kv_in, st_in)
    kv_out[...] = total
    st_out[0:1, :] = squares
    st_out[1:2, :] = largest
    q_out[...] = q_sum(xs, [[w_now[i, j] for j in range(n)] for i in range(m)], q_in)
    for c in copies:
        c.wait()


def arrivals_call(kernel, out_shape, info, xs, hbm_args, rest, flops, aliases=None, scratch=()):
    vmem = pl.BlockSpec(memory_space=pltpu.VMEM)
    smem = pl.BlockSpec(memory_space=pltpu.SMEM)
    hbm = pl.BlockSpec(memory_space=pltpu.HBM)
    return pl.pallas_call(
        kernel,
        out_shape=out_shape,
        in_specs=[smem] + [vmem] * len(xs) + [hbm] * len(hbm_args) + [vmem] * len(rest),
        out_specs=tuple(vmem for _ in out_shape),
        scratch_shapes=list(scratch),
        input_output_aliases=aliases or {},
        compiler_params=pltpu.CompilerParams(vmem_limit_bytes=RING_VMEM),
        cost_estimate=pl.CostEstimate(flops=flops, bytes_accessed=10**6, transcendentals=0),
    )(info, *xs, *hbm_args, *rest)


def matmul(half, info, shifts, next_shifts, xs, w_now, w_all, kv_all, acc):
    m = len(xs)
    out_shape = (
        jax.ShapeDtypeStruct((half, w_all.shape[2]), F32),
        jax.ShapeDtypeStruct((kv_all.shape[1], half), F32),
        jax.ShapeDtypeStruct((8, half), F32),
        jax.ShapeDtypeStruct(w_now.shape, w_now.dtype),
    )
    return arrivals_call(
        lambda *refs: matmul_kernel(shifts, next_shifts, *refs),
        out_shape,
        info,
        [*xs, w_now],
        [w_all],
        [kv_all, *acc],
        2 * m * xs[0].shape[0] * xs[0].shape[1] * 288,
        {4 + m + i: i for i in range(len(acc))},
        [pltpu.SemaphoreType.DMA((m,))],
    )


def last_kv_kernel(d, shifts, info, *refs):
    m = len(shifts)
    xs, kv_all = refs[:m], refs[m]
    kv_in, st_in, kvscale, kcos, ksin, kvt, st_out = refs[m + 1 :]
    kvs = blocks_from(info, shifts, kv_all, xs[0].shape[0] // xs[0].shape[1])
    t, squares, largest = kv_rows(xs, kvs, kv_in, st_in)
    st_out[0:1, :] = squares
    st_out[1:2, :] = largest
    t = t * (1.0 / jnp.sqrt(squares / d + norm_eps))
    first = info[0] == 0
    mk, mv, ok, ov = t[0:8], t[8:16], t[16:24], t[24:32]
    a = jnp.concatenate([jnp.where(first, mk, ok), jnp.where(first, ok, mk)], axis=0)
    b = jnp.concatenate([jnp.where(first, mv, ov), jnp.where(first, ov, mv)], axis=0)
    a = a * kvscale[:16, :]
    b = b * kvscale[16:, :]
    row = lax.broadcasted_iota(jnp.int32, a.shape, 0)
    swapped = jnp.where(row % 2 == 0, -pltpu.roll(a, a.shape[0] - 1, 0), pltpu.roll(a, 1, 0))
    a = a * kcos[...] + swapped * ksin[...]
    both = jnp.concatenate([a, b], axis=0).astype(BF16)
    for s in range(kvt.shape[0]):
        kvt[s] = both


def last_kv(d, copies, info, shifts, xs, kv_all, kv, st, kvscale, kcos, ksin):
    out_shape = (
        jax.ShapeDtypeStruct((copies,) + kv.shape, BF16),
        jax.ShapeDtypeStruct(st.shape, F32),
    )
    return arrivals_call(
        lambda *refs: last_kv_kernel(d, shifts, *refs),
        out_shape,
        info,
        xs,
        [],
        [kv_all, kv, st, kvscale, kcos, ksin],
        10**9,
    )


def last_q_kernel(d, shifts, info, *refs):
    m = len(shifts)
    xs, w_now = refs[:m], refs[m]
    q_in, st, wscale, cosine, sine, mine, msg = refs[m + 1 :]
    n = w_now.shape[1]
    q = q_sum(xs, [[w_now[i, j] for j in range(n)] for i in range(m)], q_in)
    half = q.shape[0]
    squares, largest = st[0:1, :], st[1:2, :]
    inv = columns_of(1.0 / jnp.sqrt(squares / d + norm_eps), 128)
    mine[...] = turn(q[:, :128] * inv * wscale[...], cosine[...], sine[...]).astype(BF16)
    msg[:half, :] = q[:, 128:] * inv
    msg[half:, :] = jnp.concatenate(
        [
            squares[:, :128],
            squares[:, 128:],
            largest[:, :128],
            largest[:, 128:],
            jnp.zeros((4, 128), F32),
        ],
        axis=0,
    )


def last_q(d, info, shifts, xs, w_now, q, st, wscale, cosine, sine):
    half = q.shape[0]
    out_shape = (
        jax.ShapeDtypeStruct((half, HD), BF16),
        jax.ShapeDtypeStruct((half + 8, HD), F32),
    )
    return arrivals_call(
        lambda *refs: last_q_kernel(d, shifts, *refs),
        out_shape,
        info,
        [*xs, w_now],
        [],
        [q, st, wscale, cosine, sine],
        10**9,
    )


def turn(v, cosine, sine):
    lane = lax.broadcasted_iota(jnp.int32, v.shape, 1)
    width = v.shape[1]
    swapped = jnp.where(
        lane % 2 == 0, -pltpu.roll(v, width - 1, 1), pltpu.roll(v, 1, 1)
    )
    return v * cosine + swapped * sine


def columns_of(row, width):
    return jnp.transpose(jnp.broadcast_to(row, (width, row.shape[1])))


def token_kernel(d, core, mine, msg, st, hidden, gain, wscale, cosine, sine, queries, payload, scale):
    half = mine.shape[0]
    c = core[0]
    own = pl.ds(pl.multiple_of(c * half, half), half)
    far = pl.ds(pl.multiple_of((1 - c) * half, half), half)
    queries[own, :] = mine[...]
    queries[far, :] = turn(msg[:half, :] * wscale[...], cosine[...], sine[...]).astype(BF16)
    wide = lambda r: jnp.concatenate(
        [msg[half + r : half + r + 1], msg[half + r + 1 : half + r + 2]], axis=1
    )
    for rows, squares, largest, place in (
        (own, st[0:1, :], st[1:2, :], c),
        (far, wide(0), wide(2), 1 - c),
    ):
        inverse = 1.0 / jnp.sqrt(squares / d + norm_eps)
        row_scale = largest * inverse + tiny_eps
        scale[pl.ds(2 * place, 1), :] = row_scale[:, :128]
        scale[pl.ds(2 * place + 1, 1), :] = row_scale[:, 128:]
        inv = columns_of(inverse, 128)
        rs = columns_of(row_scale, 128)
        normed = hidden[rows, :].astype(F32) * gain[...] * inv
        payload[rows, :] = (normed / rs).astype(BF16)


def head_kernel(order, kvr, keys, values, whole):
    half = kvr.shape[2]
    chips = kvr.shape[0] // 2
    n = KV_COLS_DEV
    for part in range(2):
        at = slice(part * half, (part + 1) * half)
        for i in range(chips):
            rows = kvr[2 * i + part].astype(F32)
            for which in range(2):
                for slot in range(2):
                    to = pl.ds(pl.multiple_of(order[2 * i + slot] * n, n), n)
                    lo = (2 * which + slot) * n
                    whole[which, to, :] = rows[lo : lo + n]
        for which, out in enumerate((keys, values)):
            out[at, :] = jnp.transpose(whole[which]).astype(BF16)


def call(kernel, out_shape, core, *args, flops=0, scratch=()):
    return pl.pallas_call(
        kernel,
        out_shape=out_shape,
        in_specs=[pl.BlockSpec(memory_space=pltpu.SMEM)]
        + [pl.BlockSpec(memory_space=pltpu.VMEM)] * len(args),
        scratch_shapes=list(scratch),
        compiler_params=pltpu.CompilerParams(vmem_limit_bytes=VMEM),
        cost_estimate=pl.CostEstimate(flops=flops or 10**8, bytes_accessed=10**6, transcendentals=0),
    )(core, *args)


def solution(mesh):
    tp = mesh.shape["tp"]
    side = math.isqrt(tp // 2)
    row = 2 * side

    def index(y, x, c):
        return (y % side) * row + (x % side) * 2 + c

    everyone = [(y, x, c) for y in range(side) for x in range(side) for c in range(2)]
    to_partner = [(index(y, x, c), index(y, x, 1 - c)) for y, x, c in everyone]
    heads = tp * KV_COLS_DEV // HD
    columns = side // 2

    def home(j):
        y, x = j // row, (j // 2) % side
        return index(j % heads, x - 1 + (y + x) % columns, y // columns)

    to_row = [(j, home(j)) for j in range(tp)]
    first_groups = [[index(y, x, 0) for x in range(side)] for y in range(side)]
    first_groups += [[index(y, x, 1) for y in range(side)] for x in range(side)]
    rows = [[y * row + i for i in range(row)] for y in range(side)]

    def second(v, s):
        pairs = [
            (index(y, x, c), index(y + s, x, c) if c == 0 else index(y, x + s, c))
            for y, x, c in everyone
        ]
        return lax.ppermute(v, "tp", pairs)

    def swap(v):
        return lax.ppermute(v, "tp", to_partner)

    def body(hidden, norm_gain, prefix, w_query, w_kv, w_scale):
        count, width = hidden.shape
        d = width * tp
        half = count // 2
        me = lax.axis_index("tp")
        core = me % 2
        x = (me // 2) % side
        y = me // row
        core1 = core[None].astype(jnp.int32)
        gain = norm_gain[None, :]

        def piece_at(xs, slot):
            base = y // 2
            h = jnp.where((xs - base + 1) % side < columns, 0, 1)
            source = base + columns * h
            o = (xs - source + 1) % side
            return 2 * ((o - source) % columns + columns * slot) + h

        blk = jax.ShapeDtypeStruct((half + STAT, width), BF16)
        keep, send = call(prep_kernel, (blk, blk), core1, hidden, gain)
        recv = swap(send)
        kvs = w_scale[HD:]
        hi = kvs.astype(BF16)
        mid = kvs - hi.astype(F32)
        mid, lo = mid.astype(BF16), (mid - mid.astype(BF16).astype(F32)).astype(BF16)
        scales = jnp.pad(jnp.stack([hi, mid, lo], axis=1), ((0, 0), (0, 125)))
        kv_mine = lax.ppermute(jnp.concatenate([w_kv, scales], axis=1), "tp", to_row)
        wq_other = swap(w_query)
        slots = call(
            combine_kernel,
            jax.ShapeDtypeStruct((side, half + STAT, 2 * width), BF16),
            core1,
            keep,
            recv,
        )
        gathered = lax.all_to_all(
            slots, "tp", split_axis=0, concat_axis=0, tiled=False, axis_index_groups=first_groups
        )
        positions = (prefix[0] + jnp.arange(count, dtype=jnp.int32)).astype(F32)
        pos_own = lax.dynamic_slice_in_dim(positions, core * half, half)
        pos_far = lax.dynamic_slice_in_dim(positions, (1 - core) * half, half)

        def freq(columns):
            pair = (columns % HD // 2).astype(F32)
            return jnp.power(F32(rope_base), -(2.0 * pair) / HD)

        fq = freq(jnp.arange(HD, dtype=jnp.int32))
        ang_own = pos_own[:, None] * fq[None, :]
        ang_far = pos_far[:, None] * fq[None, :]
        slots_of = jnp.arange(2 * KV_COLS_DEV, dtype=jnp.int32)
        fk = freq(piece_at(x, slots_of // KV_COLS_DEV) * KV_COLS_DEV + slots_of % KV_COLS_DEV)
        seats = jnp.arange(row, dtype=jnp.int32)
        order = piece_at(seats // 2, seats % 2).astype(jnp.int32)
        ang_k = fk[:, None] * pos_own[None, :]
        qscale = w_scale[None, :HD]
        tables = (
            jnp.cos(ang_own),
            jnp.sin(ang_own),
            jnp.cos(ang_far),
            jnp.sin(ang_far),
            jnp.cos(ang_k),
            jnp.sin(ang_k),
        )
        coord = jnp.where(core == 0, y, x)

        info = jnp.stack([core, coord]).astype(jnp.int32)
        w_all = arrange_weights(
            info, w_query.reshape(-1, 2 * width, HD), wq_other.reshape(-1, 2 * width, HD)
        )
        n = side // 2
        w_now = first_weights(info, [(0, 0), (0, 1)], w_all, n)
        gathered, w_all, w_now, tables, info, order, qscale = lax.optimization_barrier(
            (gathered, w_all, w_now, tables, info, order, qscale)
        )
        cos_own, sin_own, cos_far, sin_far, cos_k, sin_k = tables

        n = side // 2
        low = gathered[:n, :half].reshape(n * half, -1)
        high = pl.pallas_call(
            high_kernel,
            out_shape=jax.ShapeDtypeStruct((n * half + STAT, gathered.shape[2]), BF16),
            compiler_params=pltpu.CompilerParams(vmem_limit_bytes=VMEM),
            cost_estimate=pl.CostEstimate(flops=10**8, bytes_accessed=10**6, transcendentals=0),
        )(gathered)

        last_round = side // 2
        plan = [[(0, 0), (0, 1)]]
        plan += [[(r, k), (-r, k)] for r in range(1, last_round) for k in range(2)]
        plan += [[(last_round, 0), (-last_round, 1)]]

        def mm(at, acc, w_now, xs):
            *acc, w_next = matmul(
                half, info, plan[at], plan[at + 1], xs, w_now, w_all, kv_all, acc
            )
            return acc, w_next

        up, down = [second(low, 1)], [second(low, -1)]
        up.append(second(high, 1))
        down.append(second(high, -1))
        kv_other = swap(kv_mine)
        kv_all, kvscale = call(
            kv_weights_kernel,
            (
                jax.ShapeDtypeStruct((d // (2 * width), 4 * KV_COLS_DEV, 2 * width), BF16),
                jax.ShapeDtypeStruct((4 * KV_COLS_DEV, half), F32),
            ),
            info,
            kv_mine,
            kv_other,
        )
        acc, w_now = mm(0, (), w_now, [low, high])
        at = 1
        for r in range(1, last_round):
            for k in range(2):
                xs = [up[k], down[k]]
                up[k], down[k], acc = lax.optimization_barrier((up[k], down[k], acc))
                if r + 1 < last_round:
                    up[k], down[k] = second(up[k], 1), second(down[k], -1)
                elif k == 0:
                    up[k] = second(up[k], 1)
                else:
                    down[k] = second(down[k], -1)
                acc, w_now = mm(at, acc, w_now, xs)
                at += 1
        xs = [up[0], down[1]]
        shifts = plan[-1]
        kvt, st = last_kv(
            d, row, info, shifts, xs, kv_all, acc[1], acc[2], kvscale, cos_k, sin_k
        )
        kvr = lax.all_to_all(
            kvt, "tp", split_axis=0, concat_axis=0, tiled=False, axis_index_groups=rows
        )
        mine, msg = last_q(d, info, shifts, xs, w_now, acc[0], st, qscale, cos_own, sin_own)
        far = swap(msg)
        out = jax.ShapeDtypeStruct((count, HD), BF16)
        queries, payload, scale = call(
            lambda *r: token_kernel(d, *r),
            (out, out, jax.ShapeDtypeStruct((count // HD, HD), F32)),
            info,
            mine,
            far,
            st,
            hidden,
            gain,
            qscale,
            cos_far,
            sin_far,
        )
        keys, values = call(
            head_kernel, (out, out), order, kvr, scratch=[pltpu.VMEM((2, HD, half), F32)]
        )
        return queries, keys, values, payload, scale.reshape(count)

    return jax.shard_map(
        body,
        mesh=mesh,
        in_specs=(P("grp", "tp"), P("tp"), P("grp"), P(None, "tp"), P("tp", None), P("tp")),
        out_specs=(P("grp", "tp"), P("grp", "tp"), P("grp", "tp"), P("grp", "tp"), P("grp")),
        check_vma=False,
    )
```

profile of v0, /device:TPU:513, one launch (start us, length us, event | category | flops | bytes accessed | tf_op | source)
XLA Modules:
  0.0 149.3 jit_solution(599991793734768935)
XLA Ops:
  0.6 20.5 %collective-permute-start.1 = (bf16[16384,128]{1,0:T(8,128)(2,1)}, bf16[16384,128]{1,0:T(8,128)(2,1)}, u32[]{:S(2)}, u32[]{:S(2)}) collective-permute-start(bf16[16384,128]{1,0:T(8,128)(2,1)} %param.9), channel_id=1, source_target_pairs={{0,1},{1,0},{2,3},{3,2},{4,5},{5,4},{6,7},{7,6},{8,9},{9,8},{10,11... | collective-permute-start | bytes 12582920 | tf_op jit(solution)/shard_map/ppermute | solution.py:464
  21.2 0.9 copy-done.2
  22.1 0.7 copy-done.5
  22.7 0.2 shard_map.101
  22.9 0.2 collective-permute-start
  23.1 0.7 convert_bitcast_fusion.2
  23.8 0.7 convert_bitcast_fusion.1
  24.5 0.1 copy.32
  24.6 3.7 %collective-permute-done.recv = bf16[272,128]{1,0:T(8,128)(2,1)S(1)} collective-permute-done((bf16[272,128]{1,0:T(8,128)(2,1)S(1)}, bf16[272,128]{1,0:T(8,128)(2,1)S(1)}, u32[]{:S(2)}, u32[]{:S(2)}) %collective-permute-start) | collective-permute-done | bytes 69664 | tf_op jit(solution)/shard_map/ppermute | solution.py:464
  28.3 1.1 shard_map.102
  29.4 3.9 %all-to-all-start = ((bf16[8,272,256]{2,1,0:T(8,128)(2,1)}), bf16[8,272,256]{2,1,0:T(8,128)(2,1)S(1)}, u32[]{:S(2)}, u32[]{:S(2)}) async-start(bf16[8,272,256]{2,1,0:T(8,128)(2,1)} %shard_map.102), calls=%async_computation | async-start | bytes 2228224 | tf_op jit(solution)/shard_map/all_to_all | solution.py:501
  33.4 0.0 copy-start.10
  33.4 0.1 collective-permute-start.4
  34.4 0.1 fusion.17
  34.5 0.6 pad_add_fusion.info.refs_0_.core.r_0_
  35.1 0.1 multiply_sine_fusion.2
  35.2 1.6 %multiply_sine_fusion = (f32[256,128]{1,0:T(8,128)S(1)}, f32[256,128]{1,0:T(8,128)S(1)}, f32[256,128]{1,0:T(8,128)}, f32[256,128]{1,0:T(8,128)}) fusion(f32[256]{0:T(256)S(1)} %get-tuple-element.167, f32[128]{0:T(128)S(1)} %multiply_power_fusion.1, f32[256]{0:T(256)S(1)} %get-tuple-element.168), kind=kLoop, calls=%fused_computation.3 | loop fusion | flops 65536 | bytes 526848 | tf_op jit(solution)/shard_map/sin | solution.py:525
  36.8 25.8 %collective-permute-done.4.kv = bf16[16,16512]{1,0:T(8,128)(2,1)S(1)} collective-permute-done((bf16[16,16512]{1,0:T(8,128)(2,1)S(1)}, bf16[16,16512]{1,0:T(8,128)(2,1)S(1)}, u32[]{:S(2)}, u32[]{:S(2)}) %collective-permute-start.4) | collective-permute-done | bytes 528416 | tf_op jit(solution)/shard_map/ppermute | solution.py:492
  62.6 1.7 %collective-permute-start.5 = (bf16[16,16512]{1,0:T(8,128)(2,1)S(1)}, bf16[16,16512]{1,0:T(8,128)(2,1)S(1)}, u32[]{:S(2)}, u32[]{:S(2)}) collective-permute-start(bf16[16,16512]{1,0:T(8,128)(2,1)S(1)} %collective-permute-done.4.kv), channel_id=1, source_target_pairs={{0,1},{1,0},{2,3},{3,2},{4,5},{5,4},{6,7},{7,6},{8,9},{9,8},{10,11... | collective-permute-start | bytes 1585160 | tf_op jit(solution)/shard_map/ppermute | solution.py:464
  64.3 0.0 collective-permute-done.1
  64.3 8.9 %shard_map.103.refs_1_.refs_4_ = bf16[64,256,256]{2,1,0:T(8,128)(2,1)} custom-call(s32[2]{0:T(128)} %pad_add_fusion.info.refs_0_.core.r_0_, bf16[64,256,128]{2,1,0:T(8,128)(2,1)} %bitcast.22, bf16[64,256,128]{2,1,0:T(8,128)(2,1)} %bitcast.4.wo), custom_call_target="tpu_custom_call" | custom-call | flops 1000000000 | bytes 20000000 | tf_op jit(solution)/shard_map/pallas_call | solution.py:108
  73.2 1.8 %shard_map.104.refs_3_ = bf16[2,4,256,256]{3,2,1,0:T(8,128)(2,1)S(1)} custom-call(s32[2]{0:T(128)S(1)} %copy-done.4, bf16[64,256,256]{2,1,0:T(8,128)(2,1)} %shard_map.103.refs_1_.refs_4_), custom_call_target="tpu_custom_call" | custom-call | flops 100000000 | bytes 1000000 | tf_op jit(solution)/shard_map/pallas_call | solution.py:219
  75.0 0.0 all-to-all-done.gathered
  75.1 0.1 collective-permute-start.2
  75.2 2.6 %collective-permute-start.3 = (bf16[1024,256]{1,0:T(8,128)(2,1)S(1)}, bf16[1024,256]{1,0:T(8,128)(2,1)S(1)}, u32[]{:S(2)}, u32[]{:S(2)}) collective-permute-start(bf16[1024,256]{1,0:T(8,128)(2,1)S(1)} %bitcast.18), channel_id=1, source_target_pairs={{0,112},{1,15},{2,114},{3,1},{4,116},{5,3},{6,118},{7,5},{8,120},{... | collective-permute-start | bytes 1572872 | tf_op jit(solution)/shard_map/ppermute | solution.py:461
  77.8 0.1 shard_map.105.refs_2_
  77.9 0.1 collective-permute-start.8
  78.0 2.6 %collective-permute-start.9 = (bf16[1040,256]{1,0:T(8,128)(2,1)S(1)}, bf16[1040,256]{1,0:T(8,128)(2,1)S(1)}, u32[]{:S(2)}, u32[]{:S(2)}) collective-permute-start(bf16[1040,256]{1,0:T(8,128)(2,1)S(1)} %shard_map.105.refs_2_), channel_id=1, source_target_pairs={{0,112},{1,15},{2,114},{3,1},{4,116},{5,3},{6,118},{7,5},{8,120},{... | collective-permute-start | bytes 1597448 | tf_op jit(solution)/shard_map/ppermute | solution.py:461
  80.7 0.0 collective-permute-done.5.ko
  80.7 0.7 shard_map.106
  81.4 2.3 %shard_map.107 = (f32[256,256]{1,0:T(8,128)S(1)}, f32[32,256]{1,0:T(8,128)S(1)}, f32[8,256]{1,0:T(8,128)S(1)}, bf16[2,4,256,256]{3,2,1,0:T(8,128)(2,1)S(1)}) custom-call(s32[2]{0:T(128)S(1)} %copy-done.4, bf16[1024,256]{1,0:T(8,128)(2,1)S(1)} %bitcast.19, bf16[1040,256]{1,0:T(8,128)(2,1)S(1)} %shard_map.105.refs_2_, ...), custom_call_target="tpu_custom_call" | custom-call | flops 301989888 | bytes 1000000 | tf_op jit(solution)/shard_map/pallas_call | solution.py:256
  83.7 1.0 collective-permute-done.2.refs_1_
  84.7 2.7 %collective-permute-start.7 = (bf16[1024,256]{1,0:T(8,128)(2,1)S(1)}, bf16[1024,256]{1,0:T(8,128)(2,1)S(1)}, u32[]{:S(2)}, u32[]{:S(2)}) collective-permute-start(bf16[1024,256]{1,0:T(8,128)(2,1)S(1)} %collective-permute-done.3.refs_2_), channel_id=1, source_target_pairs={{0,112},{1,15},{2,114},{3,1},{4,116},{5,3},{6,118},{7,5},{8,120},{... | collective-permute-start | bytes 1572872 | tf_op jit(solution)/shard_map/ppermute | solution.py:461
  87.4 2.3 %shard_map.108 = (f32[256,256]{1,0:T(8,128)S(1)}, f32[32,256]{1,0:T(8,128)S(1)}, f32[8,256]{1,0:T(8,128)S(1)}, bf16[2,4,256,256]{3,2,1,0:T(8,128)(2,1)S(1)}) custom-call(s32[2]{0:T(128)S(1)} %copy-done.4, bf16[1024,256]{1,0:T(8,128)(2,1)S(1)} %collective-permute-done.2.refs_1_, ...), custom_call_target="tpu_custom_call", output_to_operand_aliasing={{0}: (6, {}), {1}: (7, {}), {2}: (8, {})} | custom-call | flops 301989888 | bytes 1000000 | tf_op jit(solution)/shard_map/pallas_call | solution.py:256
  89.6 0.8 collective-permute-done.8.refs_1_
  90.4 0.0 collective-permute-done.9.refs_2_
  90.4 0.0 collective-permute-start.12
  90.4 2.7 %collective-permute-start.13 = (bf16[1040,256]{1,0:T(8,128)(2,1)S(1)}, bf16[1040,256]{1,0:T(8,128)(2,1)S(1)}, u32[]{:S(2)}, u32[]{:S(2)}) collective-permute-start(bf16[1040,256]{1,0:T(8,128)(2,1)S(1)} %collective-permute-done.9.refs_2_), channel_id=1, source_target_pairs={{0,112},{1,15},{2,114},{3,1},{4,116},{5,3},{6,118},{7,5},{8,120},{... | collective-permute-start | bytes 1597448 | tf_op jit(solution)/shard_map/ppermute | solution.py:461
  93.1 2.3 %shard_map.109 = (f32[256,256]{1,0:T(8,128)S(1)}, f32[32,256]{1,0:T(8,128)S(1)}, f32[8,256]{1,0:T(8,128)S(1)}, bf16[2,4,256,256]{3,2,1,0:T(8,128)(2,1)S(1)}) custom-call(s32[2]{0:T(128)S(1)} %copy-done.4, bf16[1040,256]{1,0:T(8,128)(2,1)S(1)} %collective-permute-done.8.refs_1_, ...), custom_call_target="tpu_custom_call", output_to_operand_aliasing={{0}: (6, {}), {1}: (7, {}), {2}: (8, {})} | custom-call | flops 306708480 | bytes 1000000 | tf_op jit(solution)/shard_map/pallas_call | solution.py:256
  95.4 0.7 collective-permute-done.6.refs_1_
  96.0 2.7 %collective-permute-start.11 = (bf16[1024,256]{1,0:T(8,128)(2,1)S(1)}, bf16[1024,256]{1,0:T(8,128)(2,1)S(1)}, u32[]{:S(2)}, u32[]{:S(2)}) collective-permute-start(bf16[1024,256]{1,0:T(8,128)(2,1)S(1)} %collective-permute-done.7.refs_2_), channel_id=1, source_target_pairs={{0,112},{1,15},{2,114},{3,1},{4,116},{5,3},{6,118},{7,5},{8,120},{... | collective-permute-start | bytes 1572872 | tf_op jit(solution)/shard_map/ppermute | solution.py:461
  98.7 2.3 %shard_map.110 = (f32[256,256]{1,0:T(8,128)S(1)}, f32[32,256]{1,0:T(8,128)S(1)}, f32[8,256]{1,0:T(8,128)S(1)}, bf16[2,4,256,256]{3,2,1,0:T(8,128)(2,1)S(1)}) custom-call(s32[2]{0:T(128)S(1)} %copy-done.4, bf16[1024,256]{1,0:T(8,128)(2,1)S(1)} %collective-permute-done.6.refs_1_, ...), custom_call_target="tpu_custom_call", output_to_operand_aliasing={{0}: (6, {}), {1}: (7, {}), {2}: (8, {})} | custom-call | flops 301989888 | bytes 1000000 | tf_op jit(solution)/shard_map/pallas_call | solution.py:256
  101.0 0.8 collective-permute-done.12.refs_1_
  101.7 0.0 collective-permute-done.13.refs_2_
  101.7 0.0 collective-permute-start.15
  101.7 2.7 %collective-permute-start.16 = (bf16[1040,256]{1,0:T(8,128)(2,1)S(1)}, bf16[1040,256]{1,0:T(8,128)(2,1)S(1)}, u32[]{:S(2)}, u32[]{:S(2)}) collective-permute-start(bf16[1040,256]{1,0:T(8,128)(2,1)S(1)} %collective-permute-done.13.refs_2_), channel_id=1, source_target_pairs={{0,112},{1,15},{2,114},{3,1},{4,116},{5,3},{6,118},{7,5},{8,120},{... | collective-permute-start | bytes 1597448 | tf_op jit(solution)/shard_map/ppermute | solution.py:461
  104.4 2.3 %shard_map.111 = (f32[256,256]{1,0:T(8,128)S(1)}, f32[32,256]{1,0:T(8,128)S(1)}, f32[8,256]{1,0:T(8,128)S(1)}, bf16[2,4,256,256]{3,2,1,0:T(8,128)(2,1)S(1)}) custom-call(s32[2]{0:T(128)S(1)} %copy-done.4, bf16[1040,256]{1,0:T(8,128)(2,1)S(1)} %collective-permute-done.12.refs_1_, ...), custom_call_target="tpu_custom_call", output_to_operand_aliasing={{0}: (6, {}), {1}: (7, {}), {2}: (8, {})} | custom-call | flops 306708480 | bytes 1000000 | tf_op jit(solution)/shard_map/pallas_call | solution.py:256
  106.7 0.7 collective-permute-done.10.refs_1_
  107.4 2.3 %shard_map.112 = (f32[256,256]{1,0:T(8,128)S(1)}, f32[32,256]{1,0:T(8,128)S(1)}, f32[8,256]{1,0:T(8,128)S(1)}, bf16[2,4,256,256]{3,2,1,0:T(8,128)(2,1)S(1)}) custom-call(s32[2]{0:T(128)S(1)} %copy-done.4, bf16[1024,256]{1,0:T(8,128)(2,1)S(1)} %collective-permute-done.10.refs_1_, ...), custom_call_target="tpu_custom_call", output_to_operand_aliasing={{0}: (6, {}), {1}: (7, {}), {2}: (8, {})} | custom-call | flops 301989888 | bytes 1000000 | tf_op jit(solution)/shard_map/pallas_call | solution.py:256
  109.6 3.4 %collective-permute-done.15.refs_1_ = bf16[1040,256]{1,0:T(8,128)(2,1)S(1)} collective-permute-done((bf16[1040,256]{1,0:T(8,128)(2,1)S(1)}, bf16[1040,256]{1,0:T(8,128)(2,1)S(1)}, u32[]{:S(2)}, u32[]{:S(2)}) %collective-permute-start.15) | collective-permute-done | bytes 532512 | tf_op jit(solution)/shard_map/ppermute | solution.py:461
  113.1 0.0 collective-permute-done.16.refs_2_
  113.1 2.4 %collective-permute-start.17 = (bf16[1040,256]{1,0:T(8,128)(2,1)S(1)}, bf16[1040,256]{1,0:T(8,128)(2,1)S(1)}, u32[]{:S(2)}, u32[]{:S(2)}) collective-permute-start(bf16[1040,256]{1,0:T(8,128)(2,1)S(1)} %collective-permute-done.16.refs_2_), channel_id=1, source_target_pairs={{0,112},{1,15},{2,114},{3,1},{4,116},{5,3},{6,118},{7,5},{8,120},{... | collective-permute-start | bytes 1597448 | tf_op jit(solution)/shard_map/ppermute | solution.py:461
  115.4 2.2 %shard_map.113 = (f32[256,256]{1,0:T(8,128)S(1)}, f32[32,256]{1,0:T(8,128)S(1)}, f32[8,256]{1,0:T(8,128)S(1)}, bf16[2,4,256,256]{3,2,1,0:T(8,128)(2,1)S(1)}) custom-call(s32[2]{0:T(128)S(1)} %copy-done.4, bf16[1040,256]{1,0:T(8,128)(2,1)S(1)} %collective-permute-done.15.refs_1_, ...), custom_call_target="tpu_custom_call", output_to_operand_aliasing={{0}: (6, {}), {1}: (7, {}), {2}: (8, {})} | custom-call | flops 306708480 | bytes 1000000 | tf_op jit(solution)/shard_map/pallas_call | solution.py:256
  117.7 7.3 %collective-permute-done.14.refs_1_ = bf16[1024,256]{1,0:T(8,128)(2,1)S(1)} collective-permute-done((bf16[1024,256]{1,0:T(8,128)(2,1)S(1)}, bf16[1024,256]{1,0:T(8,128)(2,1)S(1)}, u32[]{:S(2)}, u32[]{:S(2)}) %collective-permute-start.14) | collective-permute-done | bytes 524320 | tf_op jit(solution)/shard_map/ppermute | solution.py:461
  125.0 0.0 collective-permute-done.17.refs_2_
  125.0 1.7 %shard_map.114 = (bf16[16,32,256]{2,1,0:T(8,128)(2,1)}, f32[8,256]{1,0:T(8,128)S(1)}) custom-call(s32[2]{0:T(128)S(1)} %copy-done.4, bf16[1024,256]{1,0:T(8,128)(2,1)S(1)} %collective-permute-done.14.refs_1_, bf16[1040,256]{1,0:T(8,128)(2,1)S(1)} %collective-permute-done.17.refs_2_, bf16[64,32,256]{2,1,0:T(8,128)(2,1)S(1)} %get-tuple-element.92.refs_5_.refs_3_, ...), custom_call_target="tpu_custom_call" | custom-call | flops 1000000000 | bytes 1000000 | tf_op jit(solution)/shard_map/pallas_call | solution.py:256
  126.7 9.2 %all-to-all-start.1 = ((bf16[16,32,256]{2,1,0:T(8,128)(2,1)}), bf16[16,32,256]{2,1,0:T(8,128)(2,1)S(1)}, u32[]{:S(2)}, u32[]{:S(2)}) async-start(bf16[16,32,256]{2,1,0:T(8,128)(2,1)} %get-tuple-element.162), calls=%async_computation.1 | async-start | bytes 524288 | tf_op jit(solution)/shard_map/all_to_all | solution.py:595
  135.9 1.0 copy-done.8
  136.9 1.1 shard_map.115
  138.0 0.8 collective-permute-start.18
  138.8 1.0 collective-permute-done.18.r_2_
  139.8 1.5 %shard_map.116 = (bf16[512,128]{1,0:T(8,128)(2,1)}, bf16[512,128]{1,0:T(8,128)(2,1)}, f32[4,128]{1,0:T(4,128)}) custom-call(s32[2]{0:T(128)S(1)} %copy-done.4, bf16[256,128]{1,0:T(8,128)(2,1)S(1)} %get-tuple-element.156.r_1_, f32[264,128]{1,0:T(8,128)S(1)} %collective-permute-done.18.r_2_, f32[8,256]{1,0:T(8,128)S(1)} %get-tuple-element.152.refs_5_.r_3_, ...), custom_call_target="tpu_custom_call" | custom-call | flops 100000000 | bytes 1000000 | tf_op jit(solution)/shard_map/pallas_call | solution.py:423
  141.3 6.6 %all-to-all-done.1.kvr = bf16[16,32,256]{2,1,0:T(8,128)(2,1)S(1)} async-done(((bf16[16,32,256]{2,1,0:T(8,128)(2,1)}), bf16[16,32,256]{2,1,0:T(8,128)(2,1)S(1)}, u32[]{:S(2)}, u32[]{:S(2)}) %all-to-all-start.1) | async-done | bytes 262176 | tf_op jit(solution)/shard_map/all_to_all | solution.py:595
  147.8 1.4 shard_map.117
  (32 shorter events, 0.2 us)
Async XLA Ops:
  0.6 63.7 %collective-permute-start.1 = (bf16[16384,128]{1,0:T(8,128)(2,1)}, bf16[16384,128]{1,0:T(8,128)(2,1)}, u32[]{:S(2)}, u32[]{:S(2)}) collective-permute-start(bf16[16384,128]{1,0:T(8,128)(2,1)} %param.9), channel_id=1, source_target_pairs={{0,1},{1,0},{2,3},{3,2},{4,5},{5,4},{6,7},{7,6},{8,9},{9,8},{10,11... | collective-permute-start | bytes 12582920 | tf_op jit(solution)/shard_map/ppermute | solution.py:464
  21.2 0.9 copy-start.2
  22.1 0.7 copy-start.5
  22.9 5.3 %collective-permute-start = (bf16[272,128]{1,0:T(8,128)(2,1)S(1)}, bf16[272,128]{1,0:T(8,128)(2,1)S(1)}, u32[]{:S(2)}, u32[]{:S(2)}) collective-permute-start(bf16[272,128]{1,0:T(8,128)(2,1)S(1)} %get-tuple-element.87), channel_id=1, source_target_pairs={{0,1},{1,0},{2,3},{3,2},{4,5},{5,4},{6,7},{7,6},{8,9},{9,8},{10,11... | collective-permute-start | bytes 208904 | tf_op jit(solution)/shard_map/ppermute | solution.py:464
  29.4 3.9 %copy-start.9 = (bf16[16,16384]{1,0:T(8,128)(2,1)S(1)}, bf16[16,16384]{1,0:T(8,128)(2,1)}, u32[]{:S(2)}) copy-start(bf16[16,16384]{1,0:T(8,128)(2,1)} %param.10) | copy-start | bytes 1572868
  29.4 45.6 %all-to-all-start = ((bf16[8,272,256]{2,1,0:T(8,128)(2,1)}), bf16[8,272,256]{2,1,0:T(8,128)(2,1)S(1)}, u32[]{:S(2)}, u32[]{:S(2)}) async-start(bf16[8,272,256]{2,1,0:T(8,128)(2,1)} %shard_map.102), calls=%async_computation | async-start | bytes 2228224 | tf_op jit(solution)/shard_map/all_to_all | solution.py:501
  33.4 1.2 copy-start.10
  33.4 29.2 %collective-permute-start.4 = (bf16[16,16512]{1,0:T(8,128)(2,1)S(1)}, bf16[16,16512]{1,0:T(8,128)(2,1)S(1)}, u32[]{:S(2)}, u32[]{:S(2)}) collective-permute-start(bf16[16,16512]{1,0:T(8,128)(2,1)S(1)} %fusion.1), channel_id=1, source_target_pairs={{0,14},{1,30},{2,34},{3,50},{4,70},{5,86},{6,106},{7,122},{8,6},{9... | collective-permute-start | bytes 1585160 | tf_op jit(solution)/shard_map/ppermute | solution.py:492
  62.6 18.1 %collective-permute-start.5 = (bf16[16,16512]{1,0:T(8,128)(2,1)S(1)}, bf16[16,16512]{1,0:T(8,128)(2,1)S(1)}, u32[]{:S(2)}, u32[]{:S(2)}) collective-permute-start(bf16[16,16512]{1,0:T(8,128)(2,1)S(1)} %collective-permute-done.4.kv), channel_id=1, source_target_pairs={{0,1},{1,0},{2,3},{3,2},{4,5},{5,4},{6,7},{7,6},{8,9},{9,8},{10,11... | collective-permute-start | bytes 1585160 | tf_op jit(solution)/shard_map/ppermute | solution.py:464
  64.3 8.9 %copy-start.4 = (s32[2]{0:T(128)S(1)}, s32[2]{0:T(128)}, u32[]{:S(2)}) copy-start(s32[2]{0:T(128)} %pad_add_fusion.info.refs_0_.core.r_0_) | copy-start | bytes 28
  75.1 9.7 %collective-permute-start.2 = (bf16[1024,256]{1,0:T(8,128)(2,1)S(1)}, bf16[1024,256]{1,0:T(8,128)(2,1)S(1)}, u32[]{:S(2)}, u32[]{:S(2)}) collective-permute-start(bf16[1024,256]{1,0:T(8,128)(2,1)S(1)} %bitcast.17), channel_id=1, source_target_pairs={{0,16},{1,3},{2,18},{3,5},{4,20},{5,7},{6,22},{7,9},{8,24},{9,11},... | collective-permute-start | bytes 1572872 | tf_op jit(solution)/shard_map/ppermute | solution.py:461
  75.2 9.5 %collective-permute-start.3 = (bf16[1024,256]{1,0:T(8,128)(2,1)S(1)}, bf16[1024,256]{1,0:T(8,128)(2,1)S(1)}, u32[]{:S(2)}, u32[]{:S(2)}) collective-permute-start(bf16[1024,256]{1,0:T(8,128)(2,1)S(1)} %bitcast.18), channel_id=1, source_target_pairs={{0,112},{1,15},{2,114},{3,1},{4,116},{5,3},{6,118},{7,5},{8,120},{... | collective-permute-start | bytes 1572872 | tf_op jit(solution)/shard_map/ppermute | solution.py:461
  77.9 12.5 %collective-permute-start.8 = (bf16[1040,256]{1,0:T(8,128)(2,1)S(1)}, bf16[1040,256]{1,0:T(8,128)(2,1)S(1)}, u32[]{:S(2)}, u32[]{:S(2)}) collective-permute-start(bf16[1040,256]{1,0:T(8,128)(2,1)S(1)} %shard_map.105.refs_2_), channel_id=1, source_target_pairs={{0,16},{1,3},{2,18},{3,5},{4,20},{5,7},{6,22},{7,9},{8,24},{9,11},... | collective-permute-start | bytes 1597448 | tf_op jit(solution)/shard_map/ppermute | solution.py:461
  78.0 12.4 %collective-permute-start.9 = (bf16[1040,256]{1,0:T(8,128)(2,1)S(1)}, bf16[1040,256]{1,0:T(8,128)(2,1)S(1)}, u32[]{:S(2)}, u32[]{:S(2)}) collective-permute-start(bf16[1040,256]{1,0:T(8,128)(2,1)S(1)} %shard_map.105.refs_2_), channel_id=1, source_target_pairs={{0,112},{1,15},{2,114},{3,1},{4,116},{5,3},{6,118},{7,5},{8,120},{... | collective-permute-start | bytes 1597448 | tf_op jit(solution)/shard_map/ppermute | solution.py:461
  84.7 11.3 %collective-permute-start.6 = (bf16[1024,256]{1,0:T(8,128)(2,1)S(1)}, bf16[1024,256]{1,0:T(8,128)(2,1)S(1)}, u32[]{:S(2)}, u32[]{:S(2)}) collective-permute-start(bf16[1024,256]{1,0:T(8,128)(2,1)S(1)} %collective-permute-done.2.refs_1_), channel_id=1, source_target_pairs={{0,16},{1,3},{2,18},{3,5},{4,20},{5,7},{6,22},{7,9},{8,24},{9,11},... | collective-permute-start | bytes 1572872 | tf_op jit(solution)/shard_map/ppermute | solution.py:461
  84.7 11.3 %collective-permute-start.7 = (bf16[1024,256]{1,0:T(8,128)(2,1)S(1)}, bf16[1024,256]{1,0:T(8,128)(2,1)S(1)}, u32[]{:S(2)}, u32[]{:S(2)}) collective-permute-start(bf16[1024,256]{1,0:T(8,128)(2,1)S(1)} %collective-permute-done.3.refs_2_), channel_id=1, source_target_pairs={{0,112},{1,15},{2,114},{3,1},{4,116},{5,3},{6,118},{7,5},{8,120},{... | collective-permute-start | bytes 1572872 | tf_op jit(solution)/shard_map/ppermute | solution.py:461
  90.4 11.3 %collective-permute-start.12 = (bf16[1040,256]{1,0:T(8,128)(2,1)S(1)}, bf16[1040,256]{1,0:T(8,128)(2,1)S(1)}, u32[]{:S(2)}, u32[]{:S(2)}) collective-permute-start(bf16[1040,256]{1,0:T(8,128)(2,1)S(1)} %collective-permute-done.8.refs_1_), channel_id=1, source_target_pairs={{0,16},{1,3},{2,18},{3,5},{4,20},{5,7},{6,22},{7,9},{8,24},{9,11},... | collective-permute-start | bytes 1597448 | tf_op jit(solution)/shard_map/ppermute | solution.py:461
  90.4 11.3 %collective-permute-start.13 = (bf16[1040,256]{1,0:T(8,128)(2,1)S(1)}, bf16[1040,256]{1,0:T(8,128)(2,1)S(1)}, u32[]{:S(2)}, u32[]{:S(2)}) collective-permute-start(bf16[1040,256]{1,0:T(8,128)(2,1)S(1)} %collective-permute-done.9.refs_2_), channel_id=1, source_target_pairs={{0,112},{1,15},{2,114},{3,1},{4,116},{5,3},{6,118},{7,5},{8,120},{... | collective-permute-start | bytes 1597448 | tf_op jit(solution)/shard_map/ppermute | solution.py:461
  96.0 11.3 %collective-permute-start.10 = (bf16[1024,256]{1,0:T(8,128)(2,1)S(1)}, bf16[1024,256]{1,0:T(8,128)(2,1)S(1)}, u32[]{:S(2)}, u32[]{:S(2)}) collective-permute-start(bf16[1024,256]{1,0:T(8,128)(2,1)S(1)} %collective-permute-done.6.refs_1_), channel_id=1, source_target_pairs={{0,16},{1,3},{2,18},{3,5},{4,20},{5,7},{6,22},{7,9},{8,24},{9,11},... | collective-permute-start | bytes 1572872 | tf_op jit(solution)/shard_map/ppermute | solution.py:461
  96.0 11.3 %collective-permute-start.11 = (bf16[1024,256]{1,0:T(8,128)(2,1)S(1)}, bf16[1024,256]{1,0:T(8,128)(2,1)S(1)}, u32[]{:S(2)}, u32[]{:S(2)}) collective-permute-start(bf16[1024,256]{1,0:T(8,128)(2,1)S(1)} %collective-permute-done.7.refs_2_), channel_id=1, source_target_pairs={{0,112},{1,15},{2,114},{3,1},{4,116},{5,3},{6,118},{7,5},{8,120},{... | collective-permute-start | bytes 1572872 | tf_op jit(solution)/shard_map/ppermute | solution.py:461
  101.7 11.3 %collective-permute-start.15 = (bf16[1040,256]{1,0:T(8,128)(2,1)S(1)}, bf16[1040,256]{1,0:T(8,128)(2,1)S(1)}, u32[]{:S(2)}, u32[]{:S(2)}) collective-permute-start(bf16[1040,256]{1,0:T(8,128)(2,1)S(1)} %collective-permute-done.12.refs_1_), channel_id=1, source_target_pairs={{0,16},{1,3},{2,18},{3,5},{4,20},{5,7},{6,22},{7,9},{8,24},{9,11},... | collective-permute-start | bytes 1597448 | tf_op jit(solution)/shard_map/ppermute | solution.py:461
  101.7 11.3 %collective-permute-start.16 = (bf16[1040,256]{1,0:T(8,128)(2,1)S(1)}, bf16[1040,256]{1,0:T(8,128)(2,1)S(1)}, u32[]{:S(2)}, u32[]{:S(2)}) collective-permute-start(bf16[1040,256]{1,0:T(8,128)(2,1)S(1)} %collective-permute-done.13.refs_2_), channel_id=1, source_target_pairs={{0,112},{1,15},{2,114},{3,1},{4,116},{5,3},{6,118},{7,5},{8,120},{... | collective-permute-start | bytes 1597448 | tf_op jit(solution)/shard_map/ppermute | solution.py:461
  113.1 11.9 %collective-permute-start.17 = (bf16[1040,256]{1,0:T(8,128)(2,1)S(1)}, bf16[1040,256]{1,0:T(8,128)(2,1)S(1)}, u32[]{:S(2)}, u32[]{:S(2)}) collective-permute-start(bf16[1040,256]{1,0:T(8,128)(2,1)S(1)} %collective-permute-done.16.refs_2_), channel_id=1, source_target_pairs={{0,112},{1,15},{2,114},{3,1},{4,116},{5,3},{6,118},{7,5},{8,120},{... | collective-permute-start | bytes 1597448 | tf_op jit(solution)/shard_map/ppermute | solution.py:461
  115.4 9.5 %collective-permute-start.14 = (bf16[1024,256]{1,0:T(8,128)(2,1)S(1)}, bf16[1024,256]{1,0:T(8,128)(2,1)S(1)}, u32[]{:S(2)}, u32[]{:S(2)}) collective-permute-start(bf16[1024,256]{1,0:T(8,128)(2,1)S(1)} %collective-permute-done.10.refs_1_), channel_id=1, source_target_pairs={{0,16},{1,3},{2,18},{3,5},{4,20},{5,7},{6,22},{7,9},{8,24},{9,11},... | collective-permute-start | bytes 1572872 | tf_op jit(solution)/shard_map/ppermute | solution.py:461
  125.0 1.7 %copy-start.7 = (bf16[1024,256]{1,0:T(8,128)(2,1)}, bf16[1024,256]{1,0:T(8,128)(2,1)S(1)}, u32[]{:S(2)}) copy-start(bf16[1024,256]{1,0:T(8,128)(2,1)S(1)} %collective-permute-done.14.refs_1_) | copy-start | bytes 1572868
  125.0 10.9 %copy-start = (f32[256,128]{1,0:T(8,128)S(1)}, f32[256,128]{1,0:T(8,128)}, u32[]{:S(2)}) copy-start(f32[256,128]{1,0:T(8,128)} %get-tuple-element.154.refs_7_) | copy-start | bytes 393220
  125.0 10.9 %copy-start.1 = (f32[256,128]{1,0:T(8,128)S(1)}, f32[256,128]{1,0:T(8,128)}, u32[]{:S(2)}) copy-start(f32[256,128]{1,0:T(8,128)} %get-tuple-element.155.refs_8_) | copy-start | bytes 393220
  126.7 21.2 %all-to-all-start.1 = ((bf16[16,32,256]{2,1,0:T(8,128)(2,1)}), bf16[16,32,256]{2,1,0:T(8,128)(2,1)S(1)}, u32[]{:S(2)}, u32[]{:S(2)}) async-start(bf16[16,32,256]{2,1,0:T(8,128)(2,1)} %get-tuple-element.162), calls=%async_computation.1 | async-start | bytes 524288 | tf_op jit(solution)/shard_map/all_to_all | solution.py:595
  135.9 1.0 copy-start.8
  136.9 2.8 %copy-start.3 = (bf16[512,128]{1,0:T(8,128)(2,1)S(1)}, bf16[512,128]{1,0:T(8,128)(2,1)}, u32[]{:S(2)}) copy-start(bf16[512,128]{1,0:T(8,128)(2,1)} %r_4_.1) | copy-start | bytes 393220
  136.9 2.8 %copy-start.6 = (f32[128]{0:T(128)S(1)}, f32[128]{0:T(128)}, u32[]{:S(2)}) copy-start(f32[128]{0:T(128)} %param.7) | copy-start | bytes 1540
  138.0 1.8 %collective-permute-start.18 = (f32[264,128]{1,0:T(8,128)S(1)}, f32[264,128]{1,0:T(8,128)S(1)}, u32[]{:S(2)}, u32[]{:S(2)}) collective-permute-start(f32[264,128]{1,0:T(8,128)S(1)} %get-tuple-element.157), channel_id=1, source_target_pairs={{0,1},{1,0},{2,3},{3,2},{4,5},{5,4},{6,7},{7,6},{8,9},{9,8},{10,11... | collective-permute-start | bytes 405512 | tf_op jit(solution)/shard_map/ppermute | solution.py:464
where the time goes:
time: 150 us; the launch traced here: 149 us
  starting transfers between devices  55.1 us (37%)
  waiting for transfers between devices  51.7 us (34%)
  Pallas kernels  34.2 us (23%)
  local copies, waits for them, and re-layouts  3.52 us (2%)
  other arithmetic  3.13 us (2%)
  between operations  1.66 us (1%)
    ppermute x1, waiting for transfers between devices, body(): lax.ppermute(jnp.concatenate([w_kv, scales], axis=1), 'tp', to_row)  25.8 us
    ppermute x4, starting transfers between devices, swap(): return lax.ppermute(v, 'tp', to_partner)  23.2 us
    ppermute x14, starting transfers between devices, second(): return lax.ppermute(v, 'tp', pairs)  18.7 us
    pallas_call x9, Pallas kernels, arrivals_call(): pl.pallas_call(kernel, out_shape=out_shape, in_specs=[smem] + [vmem] * le...  18.5 us
    ppermute x14, waiting for transfers between devices, second(): return lax.ppermute(v, 'tp', pairs)  14.6 us
    all_to_all x1, starting transfers between devices, body(): lax.all_to_all(kvt, 'tp', split_axis=0, concat_axis=0, tiled=False, axis_...  9.18 us
    pallas_call x1, Pallas kernels, arrange_weights(): pl.pallas_call(weights_kernel, out_shape=out, in_specs=[pl.BlockSpec(memo...  8.89 us
    all_to_all x1, waiting for transfers between devices, body(): lax.all_to_all(kvt, 'tp', split_axis=0, concat_axis=0, tiled=False, axis_...  6.58 us
  transfers between devices with their start and end apart: 21, of which 11 were waited for; matrix products, arithmetic and copies ran while one was open for 3% of the time, Pallas kernels for 21%

commit v1 on v0

--- a/solution.py
+++ b/solution.py
@@ -116,7 +116,7 @@
     )(info, wq, wo)
 
 
-def kv_weights_kernel(core, kv, ko, kv_all, kvscale):
+def kv_weights_kernel(core, kv, ko, kv_all):
     n, rows2, kb = kv_all.shape
     rows = rows2 // 2
     side = math.isqrt(n)
@@ -124,14 +124,23 @@
         at = pl.ds(pl.multiple_of(block_at(core[0], i, side) * kb, kb), kb)
         kv_all[i, :rows, :] = kv[:, at]
         kv_all[i, rows:, :] = ko[:, at]
+
+
+def kv_scale_kernel(core, kvs, kos, kvscale):
+    rows = kvs.shape[1]
     width = kvscale.shape[1]
 
     def scales(ref):
-        s = ref[:, n * kb : n * kb + 128].astype(F32)
-        s = (s[:, 0:1] + s[:, 1:2]) + s[:, 2:3]
-        return jnp.broadcast_to(s, (rows, width))
-
-    m, o = scales(kv), scales(ko)
+        shape = (rows, rows)
+        diagonal = lax.broadcasted_iota(jnp.int32, shape, 0) == lax.broadcasted_iota(
+            jnp.int32, shape, 1
+        )
+        column = jnp.sum(
+            jnp.where(diagonal, jnp.broadcast_to(ref[...], shape), 0.0), axis=1, keepdims=True
+        )
+        return jnp.broadcast_to(column, (rows, width))
+
+    m, o = scales(kvs), scales(kos)
     first = core[0] == 0
     k = rows // 2
     for j, (lo, hi) in enumerate(((0, k), (k, 2 * k))):
@@ -484,12 +493,8 @@
         blk = jax.ShapeDtypeStruct((half + STAT, width), BF16)
         keep, send = call(prep_kernel, (blk, blk), core1, hidden, gain)
         recv = swap(send)
-        kvs = w_scale[HD:]
-        hi = kvs.astype(BF16)
-        mid = kvs - hi.astype(F32)
-        mid, lo = mid.astype(BF16), (mid - mid.astype(BF16).astype(F32)).astype(BF16)
-        scales = jnp.pad(jnp.stack([hi, mid, lo], axis=1), ((0, 0), (0, 125)))
-        kv_mine = lax.ppermute(jnp.concatenate([w_kv, scales], axis=1), "tp", to_row)
+        kv_mine = lax.ppermute(w_kv, "tp", to_row)
+        kvs_mine = lax.ppermute(w_scale[None, HD:], "tp", to_row)
         wq_other = swap(w_query)
         slots = call(
             combine_kernel,
@@ -563,12 +568,9 @@
         up.append(second(high, 1))
         down.append(second(high, -1))
         kv_other = swap(kv_mine)
-        kv_all, kvscale = call(
+        kv_all = call(
             kv_weights_kernel,
-            (
-                jax.ShapeDtypeStruct((d // (2 * width), 4 * KV_COLS_DEV, 2 * width), BF16),
-                jax.ShapeDtypeStruct((4 * KV_COLS_DEV, half), F32),
-            ),
+            jax.ShapeDtypeStruct((d // (2 * width), 4 * KV_COLS_DEV, 2 * width), BF16),
             info,
             kv_mine,
             kv_other,
@@ -578,7 +580,8 @@
         for r in range(1, last_round):
             for k in range(2):
                 xs = [up[k], down[k]]
-                up[k], down[k], acc = lax.optimization_barrier((up[k], down[k], acc))
+                if at > 1:
+                    up[k], down[k], acc = lax.optimization_barrier((up[k], down[k], acc))
                 if r + 1 < last_round:
                     up[k], down[k] = second(up[k], 1), second(down[k], -1)
                 elif k == 0:
@@ -589,6 +592,14 @@
                 at += 1
         xs = [up[0], down[1]]
         shifts = plan[-1]
+        kvs_other = swap(kvs_mine)
+        kvscale = call(
+            kv_scale_kernel,
+            jax.ShapeDtypeStruct((4 * KV_COLS_DEV, half), F32),
+            info,
+            kvs_mine,
+            kvs_other,
+        )
         kvt, st = last_kv(
             d, row, info, shifts, xs, kv_all, acc[1], acc[2], kvscale, cos_k, sin_k
         )

time: 150 us -> 151 us (level)
  waiting for transfers between devices: 51.7 us -> 55.1 us
  starting transfers between devices: 55.1 us -> 52.8 us
    ppermute x1 -> x2, waiting for transfers between devices: 25.8 us -> 33.8 us  [the longest x1 25.1 us: body(): kv_mine = lax.ppermute(w_kv, 'tp', to_row)]
    ppermute x14, waiting for transfers between devices: 14.6 us -> 7.39 us  [second(): return lax.ppermute(v, 'tp', pairs)]
    all_to_all x1, starting transfers between devices: 9.18 us -> 3.69 us  [body(): lax.all_to_all(kvt, 'tp', split_axis=0, concat_axis=0, tiled=False, axis_...]
    ppermute x1 -> x2, starting transfers between devices: 0.13 us -> 3.79 us  [the longest x1 3.66 us: body(): kvs_mine = lax.ppermute(w_scale[None, HD:], 'tp', to_row)]
    ppermute x4 -> x5, waiting for transfers between devices: 4.69 us -> 7.33 us  [swap(): return lax.ppermute(v, 'tp', to_partner)]
    pallas_call x5 -> x6, Pallas kernels: 4.98 us -> 5.54 us  [call(): pl.pallas_call(kernel, out_shape=out_shape, in_specs=[pl.BlockSpec(memory...]
    ppermute x4 -> x5, starting transfers between devices: 23.2 us -> 22.9 us  [swap(): return lax.ppermute(v, 'tp', to_partner)]
  transfers between devices with their start and end apart: 21 -> 23, of which waited for: 11 -> 12; matrix products, arithmetic and copies ran while one was open for 3% -> 2% of each run, Pallas kernels for 21% -> 21%
where the time goes in v1:
time: 151 us; the launch traced here: 150 us
  waiting for transfers between devices  55.1 us (36%)
  starting transfers between devices  52.8 us (35%)
  Pallas kernels  34.8 us (23%)
  local copies, waits for them, and re-layouts  3.43 us (2%)
  other arithmetic  2.39 us (2%)
  between operations  1.69 us (1%)
    ppermute x1, waiting for transfers between devices, body(): kv_mine = lax.ppermute(w_kv, 'tp', to_row)  25.1 us
    ppermute x5, starting transfers between devices, swap(): return lax.ppermute(v, 'tp', to_partner)  22.9 us
    ppermute x14, starting transfers between devices, second(): return lax.ppermute(v, 'tp', pairs)  18.7 us
    pallas_call x9, Pallas kernels, arrivals_call(): pl.pallas_call(kernel, out_shape=out_shape, in_specs=[smem] + [vmem] * le...  18.5 us
    pallas_call x1, Pallas kernels, arrange_weights(): pl.pallas_call(weights_kernel, out_shape=out, in_specs=[pl.BlockSpec(memo...  8.89 us
    ppermute x1, waiting for transfers between devices, body(): kvs_mine = lax.ppermute(w_scale[None, HD:], 'tp', to_row)  8.67 us
    ppermute x14, waiting for transfers between devices, second(): return lax.ppermute(v, 'tp', pairs)  7.39 us
    ppermute x5, waiting for transfers between devices, swap(): return lax.ppermute(v, 'tp', to_partner)  7.33 us
  transfers between devices with their start and end apart: 23, of which 12 were waited for; matrix products, arithmetic and copies ran while one was open for 2% of the time, Pallas kernels for 21%

profile of v1, /device:TPU:513, one launch (start us, length us, event | category | flops | bytes accessed | tf_op | source)
XLA Modules:
  0.0 150.2 jit_solution(18265573636338637940)
XLA Ops:
  0.6 20.5 %collective-permute-start.1 = (bf16[16384,128]{1,0:T(8,128)(2,1)}, bf16[16384,128]{1,0:T(8,128)(2,1)}, u32[]{:S(2)}, u32[]{:S(2)}) collective-permute-start(bf16[16384,128]{1,0:T(8,128)(2,1)} %param.9), channel_id=1, source_target_pairs={{0,1},{1,0},{2,3},{3,2},{4,5},{5,4},{6,7},{7,6},{8,9},{9,8},{10,11... | collective-permute-start | bytes 12582920 | tf_op jit(solution)/shard_map/ppermute | solution.py:473
  21.2 0.9 copy-done.2
  22.1 0.7 copy-done.5
  22.7 0.2 shard_map.101
  22.9 0.2 collective-permute-start
  23.1 5.2 %collective-permute-done.recv = bf16[272,128]{1,0:T(8,128)(2,1)S(1)} collective-permute-done((bf16[272,128]{1,0:T(8,128)(2,1)S(1)}, bf16[272,128]{1,0:T(8,128)(2,1)S(1)}, u32[]{:S(2)}, u32[]{:S(2)}) %collective-permute-start) | collective-permute-done | bytes 69664 | tf_op jit(solution)/shard_map/ppermute | solution.py:473
  28.3 1.1 shard_map.102
  29.4 3.8 %all-to-all-start = ((bf16[8,272,256]{2,1,0:T(8,128)(2,1)}), bf16[8,272,256]{2,1,0:T(8,128)(2,1)S(1)}, u32[]{:S(2)}, u32[]{:S(2)}) async-start(bf16[8,272,256]{2,1,0:T(8,128)(2,1)} %shard_map.102), calls=%async_computation | async-start | bytes 2228224 | tf_op jit(solution)/shard_map/all_to_all | solution.py:506
  33.2 0.1 collective-permute-start.8
  34.2 0.1 fusion.15
  34.3 0.7 slice_bitcast_fusion.1.refs_6_.r_6_
  35.0 0.6 pad_add_fusion.info.refs_0_.core.r_0_
  35.6 0.1 multiply_sine_fusion.2
  35.7 1.6 %multiply_sine_fusion = (f32[256,128]{1,0:T(8,128)S(1)}, f32[256,128]{1,0:T(8,128)S(1)}, f32[256,128]{1,0:T(8,128)}, f32[256,128]{1,0:T(8,128)}) fusion(f32[256]{0:T(256)S(1)} %get-tuple-element.153, f32[128]{0:T(128)S(1)} %multiply_power_fusion.1, f32[256]{0:T(256)S(1)} %get-tuple-element.154), kind=kLoop, calls=%fused_computation | loop fusion | flops 65536 | bytes 526848 | tf_op jit(solution)/shard_map/sin | solution.py:530
  37.3 25.1 %collective-permute-done.8.kv = bf16[16,16384]{1,0:T(8,128)(2,1)S(1)} collective-permute-done((bf16[16,16384]{1,0:T(8,128)(2,1)}, bf16[16,16384]{1,0:T(8,128)(2,1)S(1)}, u32[]{:S(2)}, u32[]{:S(2)}) %collective-permute-start.8) | collective-permute-done | bytes 524320 | tf_op jit(solution)/shard_map/ppermute | solution.py:496
  62.4 1.7 %collective-permute-start.9 = (bf16[16,16384]{1,0:T(8,128)(2,1)S(1)}, bf16[16,16384]{1,0:T(8,128)(2,1)S(1)}, u32[]{:S(2)}, u32[]{:S(2)}) collective-permute-start(bf16[16,16384]{1,0:T(8,128)(2,1)S(1)} %collective-permute-done.8.kv), channel_id=1, source_target_pairs={{0,1},{1,0},{2,3},{3,2},{4,5},{5,4},{6,7},{7,6},{8,9},{9,8},{10,11... | collective-permute-start | bytes 1572872 | tf_op jit(solution)/shard_map/ppermute | solution.py:473
  64.1 8.9 %shard_map.103.refs_1_.refs_4_ = bf16[64,256,256]{2,1,0:T(8,128)(2,1)} custom-call(s32[2]{0:T(128)} %pad_add_fusion.info.refs_0_.core.r_0_, bf16[64,256,128]{2,1,0:T(8,128)(2,1)} %bitcast.18, bf16[64,256,128]{2,1,0:T(8,128)(2,1)} %bitcast.4.wo), custom_call_target="tpu_custom_call" | custom-call | flops 1000000000 | bytes 20000000 | tf_op jit(solution)/shard_map/pallas_call | solution.py:108
  73.0 1.8 %shard_map.104.refs_3_ = bf16[2,4,256,256]{3,2,1,0:T(8,128)(2,1)S(1)} custom-call(s32[2]{0:T(128)S(1)} %copy-done.4, bf16[64,256,256]{2,1,0:T(8,128)(2,1)} %shard_map.103.refs_1_.refs_4_), custom_call_target="tpu_custom_call" | custom-call | flops 100000000 | bytes 1000000 | tf_op jit(solution)/shard_map/pallas_call | solution.py:228
  74.7 0.0 all-to-all-done.gathered
  74.8 0.1 collective-permute-start.2
  74.9 2.6 %collective-permute-start.4 = (bf16[1024,256]{1,0:T(8,128)(2,1)S(1)}, bf16[1024,256]{1,0:T(8,128)(2,1)S(1)}, u32[]{:S(2)}, u32[]{:S(2)}) collective-permute-start(bf16[1024,256]{1,0:T(8,128)(2,1)S(1)} %bitcast.14), channel_id=1, source_target_pairs={{0,112},{1,15},{2,114},{3,1},{4,116},{5,3},{6,118},{7,5},{8,120},{... | collective-permute-start | bytes 1572872 | tf_op jit(solution)/shard_map/ppermute | solution.py:470
  77.6 0.1 shard_map.105.refs_2_
  77.6 0.1 collective-permute-start.6
  77.8 2.6 %collective-permute-start.7 = (bf16[1040,256]{1,0:T(8,128)(2,1)S(1)}, bf16[1040,256]{1,0:T(8,128)(2,1)S(1)}, u32[]{:S(2)}, u32[]{:S(2)}) collective-permute-start(bf16[1040,256]{1,0:T(8,128)(2,1)S(1)} %shard_map.105.refs_2_), channel_id=1, source_target_pairs={{0,112},{1,15},{2,114},{3,1},{4,116},{5,3},{6,118},{7,5},{8,120},{... | collective-permute-start | bytes 1597448 | tf_op jit(solution)/shard_map/ppermute | solution.py:470
  80.4 0.7 shard_map.106.refs_5_.refs_3_
  81.1 2.3 %shard_map.107 = (f32[256,256]{1,0:T(8,128)S(1)}, f32[32,256]{1,0:T(8,128)S(1)}, f32[8,256]{1,0:T(8,128)S(1)}, bf16[2,4,256,256]{3,2,1,0:T(8,128)(2,1)S(1)}) custom-call(s32[2]{0:T(128)S(1)} %copy-done.4, bf16[1024,256]{1,0:T(8,128)(2,1)S(1)} %bitcast.15, bf16[1040,256]{1,0:T(8,128)(2,1)S(1)} %shard_map.105.refs_2_, ...), custom_call_target="tpu_custom_call" | custom-call | flops 301989888 | bytes 1000000 | tf_op jit(solution)/shard_map/pallas_call | solution.py:265
  83.4 1.1 collective-permute-done.2.refs_1_
  84.4 0.0 collective-permute-start.3
  84.4 0.0 collective-permute-done.4.refs_2_
  84.4 2.7 %collective-permute-start.5 = (bf16[1024,256]{1,0:T(8,128)(2,1)S(1)}, bf16[1024,256]{1,0:T(8,128)(2,1)S(1)}, u32[]{:S(2)}, u32[]{:S(2)}) collective-permute-start(bf16[1024,256]{1,0:T(8,128)(2,1)S(1)} %collective-permute-done.4.refs_2_), channel_id=1, source_target_pairs={{0,112},{1,15},{2,114},{3,1},{4,116},{5,3},{6,118},{7,5},{8,120},{... | collective-permute-start | bytes 1572872 | tf_op jit(solution)/shard_map/ppermute | solution.py:470
  87.1 2.3 %shard_map.108 = (f32[256,256]{1,0:T(8,128)S(1)}, f32[32,256]{1,0:T(8,128)S(1)}, f32[8,256]{1,0:T(8,128)S(1)}, bf16[2,4,256,256]{3,2,1,0:T(8,128)(2,1)S(1)}) custom-call(s32[2]{0:T(128)S(1)} %copy-done.4, bf16[1024,256]{1,0:T(8,128)(2,1)S(1)} %collective-permute-done.2.refs_1_, ...), custom_call_target="tpu_custom_call", output_to_operand_aliasing={{0}: (6, {}), {1}: (7, {}), {2}: (8, {})} | custom-call | flops 301989888 | bytes 1000000 | tf_op jit(solution)/shard_map/pallas_call | solution.py:265
  89.4 0.8 collective-permute-done.6.refs_1_
  90.1 2.7 %collective-permute-start.13 = (bf16[1040,256]{1,0:T(8,128)(2,1)S(1)}, bf16[1040,256]{1,0:T(8,128)(2,1)S(1)}, u32[]{:S(2)}, u32[]{:S(2)}) collective-permute-start(bf16[1040,256]{1,0:T(8,128)(2,1)S(1)} %collective-permute-done.7.refs_2_), channel_id=1, source_target_pairs={{0,112},{1,15},{2,114},{3,1},{4,116},{5,3},{6,118},{7,5},{8,120},{... | collective-permute-start | bytes 1597448 | tf_op jit(solution)/shard_map/ppermute | solution.py:470
  92.8 2.3 %shard_map.109 = (f32[256,256]{1,0:T(8,128)S(1)}, f32[32,256]{1,0:T(8,128)S(1)}, f32[8,256]{1,0:T(8,128)S(1)}, bf16[2,4,256,256]{3,2,1,0:T(8,128)(2,1)S(1)}) custom-call(s32[2]{0:T(128)S(1)} %copy-done.4, bf16[1040,256]{1,0:T(8,128)(2,1)S(1)} %collective-permute-done.6.refs_1_, ...), custom_call_target="tpu_custom_call", output_to_operand_aliasing={{0}: (6, {}), {1}: (7, {}), {2}: (8, {})} | custom-call | flops 306708480 | bytes 1000000 | tf_op jit(solution)/shard_map/pallas_call | solution.py:265
  95.1 0.7 collective-permute-done.3.refs_1_
  95.8 0.0 collective-permute-done.5.refs_2_
  95.8 0.0 collective-permute-start.10
  95.8 2.7 %collective-permute-start.11 = (bf16[1024,256]{1,0:T(8,128)(2,1)S(1)}, bf16[1024,256]{1,0:T(8,128)(2,1)S(1)}, u32[]{:S(2)}, u32[]{:S(2)}) collective-permute-start(bf16[1024,256]{1,0:T(8,128)(2,1)S(1)} %collective-permute-done.5.refs_2_), channel_id=1, source_target_pairs={{0,112},{1,15},{2,114},{3,1},{4,116},{5,3},{6,118},{7,5},{8,120},{... | collective-permute-start | bytes 1572872 | tf_op jit(solution)/shard_map/ppermute | solution.py:470
  98.4 2.3 %shard_map.110 = (f32[256,256]{1,0:T(8,128)S(1)}, f32[32,256]{1,0:T(8,128)S(1)}, f32[8,256]{1,0:T(8,128)S(1)}, bf16[2,4,256,256]{3,2,1,0:T(8,128)(2,1)S(1)}) custom-call(s32[2]{0:T(128)S(1)} %copy-done.4, bf16[1024,256]{1,0:T(8,128)(2,1)S(1)} %collective-permute-done.3.refs_1_, ...), custom_call_target="tpu_custom_call", output_to_operand_aliasing={{0}: (6, {}), {1}: (7, {}), {2}: (8, {})} | custom-call | flops 301989888 | bytes 1000000 | tf_op jit(solution)/shard_map/pallas_call | solution.py:265
  100.7 0.8 collective-permute-done.12.refs_1_
  101.5 2.7 %collective-permute-start.16 = (bf16[1040,256]{1,0:T(8,128)(2,1)S(1)}, bf16[1040,256]{1,0:T(8,128)(2,1)S(1)}, u32[]{:S(2)}, u32[]{:S(2)}) collective-permute-start(bf16[1040,256]{1,0:T(8,128)(2,1)S(1)} %collective-permute-done.13.refs_2_), channel_id=1, source_target_pairs={{0,112},{1,15},{2,114},{3,1},{4,116},{5,3},{6,118},{7,5},{8,120},{... | collective-permute-start | bytes 1597448 | tf_op jit(solution)/shard_map/ppermute | solution.py:470
  104.1 2.3 %shard_map.111 = (f32[256,256]{1,0:T(8,128)S(1)}, f32[32,256]{1,0:T(8,128)S(1)}, f32[8,256]{1,0:T(8,128)S(1)}, bf16[2,4,256,256]{3,2,1,0:T(8,128)(2,1)S(1)}) custom-call(s32[2]{0:T(128)S(1)} %copy-done.4, bf16[1040,256]{1,0:T(8,128)(2,1)S(1)} %collective-permute-done.12.refs_1_, ...), custom_call_target="tpu_custom_call", output_to_operand_aliasing={{0}: (6, {}), {1}: (7, {}), {2}: (8, {})} | custom-call | flops 306708480 | bytes 1000000 | tf_op jit(solution)/shard_map/pallas_call | solution.py:265
  106.4 0.7 collective-permute-done.10.refs_1_
  107.1 2.3 %shard_map.112 = (f32[256,256]{1,0:T(8,128)S(1)}, f32[32,256]{1,0:T(8,128)S(1)}, f32[8,256]{1,0:T(8,128)S(1)}, bf16[2,4,256,256]{3,2,1,0:T(8,128)(2,1)S(1)}) custom-call(s32[2]{0:T(128)S(1)} %copy-done.4, bf16[1024,256]{1,0:T(8,128)(2,1)S(1)} %collective-permute-done.10.refs_1_, ...), custom_call_target="tpu_custom_call", output_to_operand_aliasing={{0}: (6, {}), {1}: (7, {}), {2}: (8, {})} | custom-call | flops 301989888 | bytes 1000000 | tf_op jit(solution)/shard_map/pallas_call | solution.py:265
  109.4 3.4 %collective-permute-done.15.refs_1_ = bf16[1040,256]{1,0:T(8,128)(2,1)S(1)} collective-permute-done((bf16[1040,256]{1,0:T(8,128)(2,1)S(1)}, bf16[1040,256]{1,0:T(8,128)(2,1)S(1)}, u32[]{:S(2)}, u32[]{:S(2)}) %collective-permute-start.15) | collective-permute-done | bytes 532512 | tf_op jit(solution)/shard_map/ppermute | solution.py:470
  112.8 2.4 %collective-permute-start.17 = (bf16[1040,256]{1,0:T(8,128)(2,1)S(1)}, bf16[1040,256]{1,0:T(8,128)(2,1)S(1)}, u32[]{:S(2)}, u32[]{:S(2)}) collective-permute-start(bf16[1040,256]{1,0:T(8,128)(2,1)S(1)} %collective-permute-done.16.refs_2_), channel_id=1, source_target_pairs={{0,112},{1,15},{2,114},{3,1},{4,116},{5,3},{6,118},{7,5},{8,120},{... | collective-permute-start | bytes 1597448 | tf_op jit(solution)/shard_map/ppermute | solution.py:470
  115.2 3.7 %collective-permute-start.18 = (f32[1,16]{1,0:T(1,128)S(1)}, f32[1,16]{1,0:T(1,128)S(1)}, u32[]{:S(2)}, u32[]{:S(2)}) collective-permute-start(f32[1,16]{1,0:T(1,128)S(1)} %slice_bitcast_fusion), channel_id=1, source_target_pairs={{0,14},{1,30},{2,34},{3,50},{4,70},{5,86},{6,106},{7,122},{8,6},{9... | collective-permute-start | bytes 200 | tf_op jit(solution)/shard_map/ppermute | solution.py:497
  118.8 8.7 %collective-permute-done.18.kvs = f32[1,16]{1,0:T(1,128)S(1)} collective-permute-done((f32[1,16]{1,0:T(1,128)S(1)}, f32[1,16]{1,0:T(1,128)S(1)}, u32[]{:S(2)}, u32[]{:S(2)}) %collective-permute-start.18) | collective-permute-done | bytes 96 | tf_op jit(solution)/shard_map/ppermute | solution.py:497
  127.5 1.2 collective-permute-done.19.kos
  128.7 0.6 shard_map.114.refs_6_
  129.3 2.2 %shard_map.113 = (f32[256,256]{1,0:T(8,128)S(1)}, f32[32,256]{1,0:T(8,128)S(1)}, f32[8,256]{1,0:T(8,128)S(1)}, bf16[2,4,256,256]{3,2,1,0:T(8,128)(2,1)S(1)}) custom-call(s32[2]{0:T(128)S(1)} %copy-done.4, bf16[1040,256]{1,0:T(8,128)(2,1)S(1)} %collective-permute-done.15.refs_1_, ...), custom_call_target="tpu_custom_call", output_to_operand_aliasing={{0}: (6, {}), {1}: (7, {}), {2}: (8, {})} | custom-call | flops 306708480 | bytes 1000000 | tf_op jit(solution)/shard_map/pallas_call | solution.py:265
  131.6 0.0 copy-start
  131.6 0.0 copy-start.1
  131.6 0.0 copy-start.3
  131.6 0.0 copy-start.6
  131.6 1.7 %shard_map.115 = (bf16[16,32,256]{2,1,0:T(8,128)(2,1)}, f32[8,256]{1,0:T(8,128)S(1)}) custom-call(s32[2]{0:T(128)S(1)} %copy-done.4, bf16[1024,256]{1,0:T(8,128)(2,1)S(1)} %collective-permute-done.14.refs_1_, bf16[1040,256]{1,0:T(8,128)(2,1)S(1)} %collective-permute-done.17.refs_2_, bf16[64,32,256]{2,1,0:T(8,128)(2,1)S(1)} %shard_map.106.refs_5_.refs_3_, ...), custom_call_target="tpu_custom_call" | custom-call | flops 1000000000 | bytes 1000000 | tf_op jit(solution)/shard_map/pallas_call | solution.py:265
  133.3 3.7 %all-to-all-start.1 = ((bf16[16,32,256]{2,1,0:T(8,128)(2,1)}), bf16[16,32,256]{2,1,0:T(8,128)(2,1)S(1)}, u32[]{:S(2)}, u32[]{:S(2)}) async-start(bf16[16,32,256]{2,1,0:T(8,128)(2,1)} %get-tuple-element.148), calls=%async_computation.1 | async-start | bytes 524288 | tf_op jit(solution)/shard_map/all_to_all | solution.py:606
  137.1 1.0 copy-done.8
  138.1 1.1 shard_map.116
  139.2 0.6 collective-permute-start.20
  139.7 1.0 collective-permute-done.20.r_2_
  140.7 1.5 shard_map.117
  142.2 6.6 %all-to-all-done.1.kvr = bf16[16,32,256]{2,1,0:T(8,128)(2,1)S(1)} async-done(((bf16[16,32,256]{2,1,0:T(8,128)(2,1)}), bf16[16,32,256]{2,1,0:T(8,128)(2,1)S(1)}, u32[]{:S(2)}, u32[]{:S(2)}) %all-to-all-start.1) | async-done | bytes 262176 | tf_op jit(solution)/shard_map/all_to_all | solution.py:606
  148.8 1.4 shard_map.118
  (31 shorter events, 0.2 us)
Async XLA Ops:
  0.6 63.4 %collective-permute-start.1 = (bf16[16384,128]{1,0:T(8,128)(2,1)}, bf16[16384,128]{1,0:T(8,128)(2,1)}, u32[]{:S(2)}, u32[]{:S(2)}) collective-permute-start(bf16[16384,128]{1,0:T(8,128)(2,1)} %param.9), channel_id=1, source_target_pairs={{0,1},{1,0},{2,3},{3,2},{4,5},{5,4},{6,7},{7,6},{8,9},{9,8},{10,11... | collective-permute-start | bytes 12582920 | tf_op jit(solution)/shard_map/ppermute | solution.py:473
  21.2 0.9 copy-start.2
  22.1 0.7 copy-start.5
  22.9 5.3 %collective-permute-start = (bf16[272,128]{1,0:T(8,128)(2,1)S(1)}, bf16[272,128]{1,0:T(8,128)(2,1)S(1)}, u32[]{:S(2)}, u32[]{:S(2)}) collective-permute-start(bf16[272,128]{1,0:T(8,128)(2,1)S(1)} %get-tuple-element.80), channel_id=1, source_target_pairs={{0,1},{1,0},{2,3},{3,2},{4,5},{5,4},{6,7},{7,6},{8,9},{9,8},{10,11... | collective-permute-start | bytes 208904 | tf_op jit(solution)/shard_map/ppermute | solution.py:473
  29.4 45.3 %all-to-all-start = ((bf16[8,272,256]{2,1,0:T(8,128)(2,1)}), bf16[8,272,256]{2,1,0:T(8,128)(2,1)S(1)}, u32[]{:S(2)}, u32[]{:S(2)}) async-start(bf16[8,272,256]{2,1,0:T(8,128)(2,1)} %shard_map.102), calls=%async_computation | async-start | bytes 2228224 | tf_op jit(solution)/shard_map/all_to_all | solution.py:506
  33.2 29.2 %collective-permute-start.8 = (bf16[16,16384]{1,0:T(8,128)(2,1)}, bf16[16,16384]{1,0:T(8,128)(2,1)S(1)}, u32[]{:S(2)}, u32[]{:S(2)}) collective-permute-start(bf16[16,16384]{1,0:T(8,128)(2,1)} %param.10), channel_id=1, source_target_pairs={{0,14},{1,30},{2,34},{3,50},{4,70},{5,86},{6,106},{7,122},{8,6},{9... | collective-permute-start | bytes 1572872 | tf_op jit(solution)/shard_map/ppermute | solution.py:496
  62.4 18.0 %collective-permute-start.9 = (bf16[16,16384]{1,0:T(8,128)(2,1)S(1)}, bf16[16,16384]{1,0:T(8,128)(2,1)S(1)}, u32[]{:S(2)}, u32[]{:S(2)}) collective-permute-start(bf16[16,16384]{1,0:T(8,128)(2,1)S(1)} %collective-permute-done.8.kv), channel_id=1, source_target_pairs={{0,1},{1,0},{2,3},{3,2},{4,5},{5,4},{6,7},{7,6},{8,9},{9,8},{10,11... | collective-permute-start | bytes 1572872 | tf_op jit(solution)/shard_map/ppermute | solution.py:473
  64.1 8.9 %copy-start.4 = (s32[2]{0:T(128)S(1)}, s32[2]{0:T(128)}, u32[]{:S(2)}) copy-start(s32[2]{0:T(128)} %pad_add_fusion.info.refs_0_.core.r_0_) | copy-start | bytes 28
  74.8 9.7 %collective-permute-start.2 = (bf16[1024,256]{1,0:T(8,128)(2,1)S(1)}, bf16[1024,256]{1,0:T(8,128)(2,1)S(1)}, u32[]{:S(2)}, u32[]{:S(2)}) collective-permute-start(bf16[1024,256]{1,0:T(8,128)(2,1)S(1)} %bitcast.13), channel_id=1, source_target_pairs={{0,16},{1,3},{2,18},{3,5},{4,20},{5,7},{6,22},{7,9},{8,24},{9,11},... | collective-permute-start | bytes 1572872 | tf_op jit(solution)/shard_map/ppermute | solution.py:470
  74.9 9.5 %collective-permute-start.4 = (bf16[1024,256]{1,0:T(8,128)(2,1)S(1)}, bf16[1024,256]{1,0:T(8,128)(2,1)S(1)}, u32[]{:S(2)}, u32[]{:S(2)}) collective-permute-start(bf16[1024,256]{1,0:T(8,128)(2,1)S(1)} %bitcast.14), channel_id=1, source_target_pairs={{0,112},{1,15},{2,114},{3,1},{4,116},{5,3},{6,118},{7,5},{8,120},{... | collective-permute-start | bytes 1572872 | tf_op jit(solution)/shard_map/ppermute | solution.py:470
  77.6 12.5 %collective-permute-start.6 = (bf16[1040,256]{1,0:T(8,128)(2,1)S(1)}, bf16[1040,256]{1,0:T(8,128)(2,1)S(1)}, u32[]{:S(2)}, u32[]{:S(2)}) collective-permute-start(bf16[1040,256]{1,0:T(8,128)(2,1)S(1)} %shard_map.105.refs_2_), channel_id=1, source_target_pairs={{0,16},{1,3},{2,18},{3,5},{4,20},{5,7},{6,22},{7,9},{8,24},{9,11},... | collective-permute-start | bytes 1597448 | tf_op jit(solution)/shard_map/ppermute | solution.py:470
  77.8 12.4 %collective-permute-start.7 = (bf16[1040,256]{1,0:T(8,128)(2,1)S(1)}, bf16[1040,256]{1,0:T(8,128)(2,1)S(1)}, u32[]{:S(2)}, u32[]{:S(2)}) collective-permute-start(bf16[1040,256]{1,0:T(8,128)(2,1)S(1)} %shard_map.105.refs_2_), channel_id=1, source_target_pairs={{0,112},{1,15},{2,114},{3,1},{4,116},{5,3},{6,118},{7,5},{8,120},{... | collective-permute-start | bytes 1597448 | tf_op jit(solution)/shard_map/ppermute | solution.py:470
  84.4 11.3 %collective-permute-start.3 = (bf16[1024,256]{1,0:T(8,128)(2,1)S(1)}, bf16[1024,256]{1,0:T(8,128)(2,1)S(1)}, u32[]{:S(2)}, u32[]{:S(2)}) collective-permute-start(bf16[1024,256]{1,0:T(8,128)(2,1)S(1)} %collective-permute-done.2.refs_1_), channel_id=1, source_target_pairs={{0,16},{1,3},{2,18},{3,5},{4,20},{5,7},{6,22},{7,9},{8,24},{9,11},... | collective-permute-start | bytes 1572872 | tf_op jit(solution)/shard_map/ppermute | solution.py:470
  84.4 11.3 %collective-permute-start.5 = (bf16[1024,256]{1,0:T(8,128)(2,1)S(1)}, bf16[1024,256]{1,0:T(8,128)(2,1)S(1)}, u32[]{:S(2)}, u32[]{:S(2)}) collective-permute-start(bf16[1024,256]{1,0:T(8,128)(2,1)S(1)} %collective-permute-done.4.refs_2_), channel_id=1, source_target_pairs={{0,112},{1,15},{2,114},{3,1},{4,116},{5,3},{6,118},{7,5},{8,120},{... | collective-permute-start | bytes 1572872 | tf_op jit(solution)/shard_map/ppermute | solution.py:470
  90.1 11.3 %collective-permute-start.12 = (bf16[1040,256]{1,0:T(8,128)(2,1)S(1)}, bf16[1040,256]{1,0:T(8,128)(2,1)S(1)}, u32[]{:S(2)}, u32[]{:S(2)}) collective-permute-start(bf16[1040,256]{1,0:T(8,128)(2,1)S(1)} %collective-permute-done.6.refs_1_), channel_id=1, source_target_pairs={{0,16},{1,3},{2,18},{3,5},{4,20},{5,7},{6,22},{7,9},{8,24},{9,11},... | collective-permute-start | bytes 1597448 | tf_op jit(solution)/shard_map/ppermute | solution.py:470
  90.1 11.3 %collective-permute-start.13 = (bf16[1040,256]{1,0:T(8,128)(2,1)S(1)}, bf16[1040,256]{1,0:T(8,128)(2,1)S(1)}, u32[]{:S(2)}, u32[]{:S(2)}) collective-permute-start(bf16[1040,256]{1,0:T(8,128)(2,1)S(1)} %collective-permute-done.7.refs_2_), channel_id=1, source_target_pairs={{0,112},{1,15},{2,114},{3,1},{4,116},{5,3},{6,118},{7,5},{8,120},{... | collective-permute-start | bytes 1597448 | tf_op jit(solution)/shard_map/ppermute | solution.py:470
  95.8 11.3 %collective-permute-start.10 = (bf16[1024,256]{1,0:T(8,128)(2,1)S(1)}, bf16[1024,256]{1,0:T(8,128)(2,1)S(1)}, u32[]{:S(2)}, u32[]{:S(2)}) collective-permute-start(bf16[1024,256]{1,0:T(8,128)(2,1)S(1)} %collective-permute-done.3.refs_1_), channel_id=1, source_target_pairs={{0,16},{1,3},{2,18},{3,5},{4,20},{5,7},{6,22},{7,9},{8,24},{9,11},... | collective-permute-start | bytes 1572872 | tf_op jit(solution)/shard_map/ppermute | solution.py:470
  95.8 11.3 %collective-permute-start.11 = (bf16[1024,256]{1,0:T(8,128)(2,1)S(1)}, bf16[1024,256]{1,0:T(8,128)(2,1)S(1)}, u32[]{:S(2)}, u32[]{:S(2)}) collective-permute-start(bf16[1024,256]{1,0:T(8,128)(2,1)S(1)} %collective-permute-done.5.refs_2_), channel_id=1, source_target_pairs={{0,112},{1,15},{2,114},{3,1},{4,116},{5,3},{6,118},{7,5},{8,120},{... | collective-permute-start | bytes 1572872 | tf_op jit(solution)/shard_map/ppermute | solution.py:470
  101.5 11.3 %collective-permute-start.15 = (bf16[1040,256]{1,0:T(8,128)(2,1)S(1)}, bf16[1040,256]{1,0:T(8,128)(2,1)S(1)}, u32[]{:S(2)}, u32[]{:S(2)}) collective-permute-start(bf16[1040,256]{1,0:T(8,128)(2,1)S(1)} %collective-permute-done.12.refs_1_), channel_id=1, source_target_pairs={{0,16},{1,3},{2,18},{3,5},{4,20},{5,7},{6,22},{7,9},{8,24},{9,11},... | collective-permute-start | bytes 1597448 | tf_op jit(solution)/shard_map/ppermute | solution.py:470
  101.5 11.3 %collective-permute-start.16 = (bf16[1040,256]{1,0:T(8,128)(2,1)S(1)}, bf16[1040,256]{1,0:T(8,128)(2,1)S(1)}, u32[]{:S(2)}, u32[]{:S(2)}) collective-permute-start(bf16[1040,256]{1,0:T(8,128)(2,1)S(1)} %collective-permute-done.13.refs_2_), channel_id=1, source_target_pairs={{0,112},{1,15},{2,114},{3,1},{4,116},{5,3},{6,118},{7,5},{8,120},{... | collective-permute-start | bytes 1597448 | tf_op jit(solution)/shard_map/ppermute | solution.py:470
  107.1 8.1 %copy-start.9 = (f32[144]{0:T(256)S(1)}, f32[144]{0:T(256)}, u32[]{:S(2)}) copy-start(f32[144]{0:T(256)} %param.11) | copy-start | bytes 1732
  112.8 18.8 %collective-permute-start.17 = (bf16[1040,256]{1,0:T(8,128)(2,1)S(1)}, bf16[1040,256]{1,0:T(8,128)(2,1)S(1)}, u32[]{:S(2)}, u32[]{:S(2)}) collective-permute-start(bf16[1040,256]{1,0:T(8,128)(2,1)S(1)} %collective-permute-done.16.refs_2_), channel_id=1, source_target_pairs={{0,112},{1,15},{2,114},{3,1},{4,116},{5,3},{6,118},{7,5},{8,120},{... | collective-permute-start | bytes 1597448 | tf_op jit(solution)/shard_map/ppermute | solution.py:470
  115.2 16.4 %collective-permute-start.14 = (bf16[1024,256]{1,0:T(8,128)(2,1)S(1)}, bf16[1024,256]{1,0:T(8,128)(2,1)S(1)}, u32[]{:S(2)}, u32[]{:S(2)}) collective-permute-start(bf16[1024,256]{1,0:T(8,128)(2,1)S(1)} %collective-permute-done.10.refs_1_), channel_id=1, source_target_pairs={{0,16},{1,3},{2,18},{3,5},{4,20},{5,7},{6,22},{7,9},{8,24},{9,11},... | collective-permute-start | bytes 1572872 | tf_op jit(solution)/shard_map/ppermute | solution.py:470
  115.2 12.3 %collective-permute-start.18 = (f32[1,16]{1,0:T(1,128)S(1)}, f32[1,16]{1,0:T(1,128)S(1)}, u32[]{:S(2)}, u32[]{:S(2)}) collective-permute-start(f32[1,16]{1,0:T(1,128)S(1)} %slice_bitcast_fusion), channel_id=1, source_target_pairs={{0,14},{1,30},{2,34},{3,50},{4,70},{5,86},{6,106},{7,122},{8,6},{9... | collective-permute-start | bytes 200 | tf_op jit(solution)/shard_map/ppermute | solution.py:497
  127.5 1.2 collective-permute-start.19
  131.6 5.5 %copy-start = (f32[256,128]{1,0:T(8,128)S(1)}, f32[256,128]{1,0:T(8,128)}, u32[]{:S(2)}) copy-start(f32[256,128]{1,0:T(8,128)} %get-tuple-element.140.refs_7_) | copy-start | bytes 393220
  131.6 5.5 %copy-start.1 = (f32[256,128]{1,0:T(8,128)S(1)}, f32[256,128]{1,0:T(8,128)}, u32[]{:S(2)}) copy-start(f32[256,128]{1,0:T(8,128)} %get-tuple-element.141.refs_8_) | copy-start | bytes 393220
  131.6 9.2 %copy-start.3 = (bf16[512,128]{1,0:T(8,128)(2,1)S(1)}, bf16[512,128]{1,0:T(8,128)(2,1)}, u32[]{:S(2)}) copy-start(bf16[512,128]{1,0:T(8,128)(2,1)} %r_4_.1) | copy-start | bytes 393220
  131.6 9.1 %copy-start.6 = (f32[128]{0:T(128)S(1)}, f32[128]{0:T(128)}, u32[]{:S(2)}) copy-start(f32[128]{0:T(128)} %param.7) | copy-start | bytes 1540
  131.6 1.7 %copy-start.7 = (bf16[1024,256]{1,0:T(8,128)(2,1)}, bf16[1024,256]{1,0:T(8,128)(2,1)S(1)}, u32[]{:S(2)}) copy-start(bf16[1024,256]{1,0:T(8,128)(2,1)S(1)} %collective-permute-done.14.refs_1_) | copy-start | bytes 1572868
  133.3 15.5 %all-to-all-start.1 = ((bf16[16,32,256]{2,1,0:T(8,128)(2,1)}), bf16[16,32,256]{2,1,0:T(8,128)(2,1)S(1)}, u32[]{:S(2)}, u32[]{:S(2)}) async-start(bf16[16,32,256]{2,1,0:T(8,128)(2,1)} %get-tuple-element.148), calls=%async_computation.1 | async-start | bytes 524288 | tf_op jit(solution)/shard_map/all_to_all | solution.py:606
  137.1 1.0 copy-start.8
  139.2 1.6 %collective-permute-start.20 = (f32[264,128]{1,0:T(8,128)S(1)}, f32[264,128]{1,0:T(8,128)S(1)}, u32[]{:S(2)}, u32[]{:S(2)}) collective-permute-start(f32[264,128]{1,0:T(8,128)S(1)} %get-tuple-element.143), channel_id=1, source_target_pairs={{0,1},{1,0},{2,3},{3,2},{4,5},{5,4},{6,7},{7,6},{8,9},{9,8},{10,11... | collective-permute-start | bytes 405512 | tf_op jit(solution)/shard_map/ppermute | solution.py:473
